TPU v7x, 32 devices: a whole 2x2x4 slice. The times are simulated.
32 devices in a mesh: root: 4 (over x, core), virt: 8 (over z, y).
Axes of the slice: x: 2, y: 2, z: 4, core: 2. Of those that a mesh axis runs over, the one named last changes fastest.
Arguments:
- r2: bfloat16 [512, 16384], P('virt', 'root'), parts along dimension 1, may hold values from -6 to 6
- tau: bfloat16 [512, 512, 3072], P('virt', None, 'root'), parts along dimension 2, may hold values from -6 to 6
- w_vvv: bfloat16 [512, 512, 512], P('virt'), may hold values from -0.01171875 to 0.01171875
- w_oooo: bfloat16 [768, 4096], P('virt'), may hold values from -0.09375 to 0.09375
- w_ovoo: bfloat16 [64, 768, 512], P(None, 'virt'), may hold values from -0.75 to 0.75
- fock_oo: bfloat16 [64, 64], replicated, may hold values from -0.75 to 0.75
- fock_vv: bfloat16 [512, 512], replicated, may hold values from -0.25 to 0.25
- r1: bfloat16 [256], P('root'), parts along dimension 0, may hold values from -6 to 6
Outputs:
- sigma: float32 [3072, 512], P(('root', 'virt')), parts along dimension 0
There are 4 independent parts, one for each index of `root`. A program takes and returns all parts, laid end to end along the dimension named above; an argument that names none is the same for every part. Nothing has to cross between parts.
All inputs are finite; a program needn't handle non-finite values.
Results may differ from a plain program's by a relative error of at most 0.0003.
Values may be sent and summed in bfloat16 or wider, within the bound.
No kernel may reach another device: no remote copies, remote signals or barrier semaphores. Data moves between devices by JAX's collectives and lax.ppermute only.
A program may use at most 256 MiB of HBM per device.

v0:
```python
import jax
import jax.numpy as jnp
from jax import lax
from jax.sharding import PartitionSpec as P


def local_terms(carried, segment, fock_vv, fock_oo, w_oooo, pair_first):
    segment_rows = segment.shape[0]
    occupied = fock_oo.shape[0]
    pair_rows = w_oooo.shape[0]
    window = lax.dynamic_slice_in_dim(segment, pair_first, pair_rows, 1)
    carried = jnp.einsum("ep,ae->pa", window, fock_vv, preferred_element_type=jnp.float32)
    cubic_view = segment.reshape(segment_rows, occupied, occupied)
    first_term = jnp.einsum("mi,amj->aij", fock_oo, cubic_view, preferred_element_type=jnp.float32)
    second_term = jnp.einsum("mj,aim->aij", fock_oo, cubic_view, preferred_element_type=jnp.float32)
    occ_part = (first_term + second_term).reshape(segment_rows, occupied * occupied)
    occ_window = lax.dynamic_slice_in_dim(occ_part, pair_first, pair_rows, 1)
    quartic = jnp.einsum("pk,ak->pa", w_oooo, segment, preferred_element_type=jnp.float32)
    update = quartic - occ_window.T
    return carried + update


def on_device(r2, tau, w_vvv, w_oooo, w_ovoo, fock_oo, fock_vv, r1):
    pair_rows = w_oooo.shape[0]
    pair_first = lax.axis_index("virt") * pair_rows
    initial = jnp.zeros((pair_rows, fock_vv.shape[0]), jnp.float32)
    folded = local_terms(
        initial,
        lax.all_gather(r2, "virt", axis=0, tiled=True),
        fock_vv,
        fock_oo,
        w_oooo,
        pair_first,
    )
    weights = lax.all_to_all(w_vvv, "virt", split_axis=1, concat_axis=0, tiled=True)
    three_virtual = lax.psum_scatter(
        jnp.einsum("bep,eba->pa", tau, weights, preferred_element_type=jnp.float32),
        "virt",
        scatter_dimension=0,
        tiled=True,
    )
    singles = jnp.dot(
        r1[None, :], w_ovoo.reshape(w_ovoo.shape[0], -1), preferred_element_type=jnp.float32
    ).reshape(pair_rows, -1)
    return three_virtual + folded - singles


def solution(mesh):
    in_specs = (
        P("virt", "root"),
        P("virt", None, "root"),
        P("virt", None, None),
        P("virt", None),
        P(None, "virt", None),
        P(),
        P(),
        P("root"),
    )
    out_specs = P(("root", "virt"), None)
    return jax.shard_map(
        on_device, mesh=mesh, in_specs=in_specs, out_specs=out_specs, check_vma=False
    )
```

profile of v0, /device:TPU:0, one launch (start us, length us, event | category | flops | bytes accessed | tf_op | source)
XLA Modules:
  0.0 951.4 jit_solution(265024146681046235)
XLA Ops:
  6.5 0.0 copy-start
  6.5 31.2 %copy.24 = bf16[64,512,512]{2,0,1:T(8,128)(2,1)} copy(bf16[64,512,512]{2,1,0:T(8,128)(2,1)} %param.10) | data formatting | bytes 67108864 | tf_op args[2]
  37.7 7.3 all-to-all-start
  45.0 0.0 all-gather.2.cloned.1.call-start
  45.0 0.7 all-gather.2.cloned.1.call-update
  45.7 0.2 reduce-scatter.2.cloned.1.call-start
  46.0 773.4 %all-to-all-done = bf16[64,512,512]{2,0,1:T(8,128)(2,1)} async-done(((bf16[64,512,512]{2,0,1:T(8,128)(2,1)}), bf16[64,512,512]{2,0,1:T(8,128)(2,1)}, u32[]{:S(2)}, u32[]{:S(2)}) %all-to-all-start) | async-done | bytes 33554464 | tf_op jit(solution)/shard_map/all_to_all | solution.py:35
  819.4 22.9 %copy.25 = bf16[64,8,64,512]{3,0,1,2:T(8,128)(2,1)} copy(bf16[64,8,64,512]{3,0,2,1:T(8,128)(2,1)} %bitcast) | data formatting | bytes 67108864 | tf_op jit(solution)/shard_map/all_to_all | solution.py:35
  842.3 0.0 copy-start.5
  842.3 35.2 %convolution_bitcast_fusion = f32[768,512]{1,0:T(8,128)} fusion(bf16[64,512,768]{2,1,0:T(8,128)(2,1)} %param.9, bf16[512,64,512]{2,0,1:T(8,128)(2,1)} %bitcast.42), kind=kOutput, calls=%fused_computation.6 | convolution fusion | flops 25769803776 | bytes 85458944 | tf_op jit(solution)/shard_map/bep,eba->pa/dot_general | solution.py:37
  877.5 0.0 reduce-scatter.2.cloned.1.call-update
  877.6 0.0 copy-done.5
  877.6 10.2 %fusion = f32[1,96,512]{2,0,1:T(1,128)} fusion(bf16[64]{0:T(256)(128)(2,1)S(1)} %copy-done.5, bf16[8,8,96,512]{3,2,1,0:T(8,128)(2,1)} %bitcast.44), kind=kOutput, calls=%fused_computation.1 | convolution fusion | flops 6291456 | bytes 6488192 | tf_op jit(solution)/shard_map/dot_general | solution.py:42
  887.7 0.0 copy-start.4
  887.7 0.0 all-gather.2.cloned.1.call-done
  887.7 6.5 copy.27
  894.2 0.0 copy-done.4
  894.2 0.0 copy-start.1
  894.2 3.8 fusion.10
  898.0 0.0 copy-done.1
  898.0 7.9 bitcast_add_fusion
  905.9 0.0 copy-start.2
  905.9 0.0 copy-start.3
  905.9 4.9 copy.32
  910.8 0.0 copy-done
  910.8 0.0 copy-done.2
  910.8 1.5 convolution_subtract_fusion
  912.3 30.1 %reduce-scatter.2.cloned.1.call-done = f32[96,512]{1,0:T(8,128)} async-done(((f32[768,512]{1,0:T(8,128)}), f32[96,512]{1,0:T(8,128)}) %reduce-scatter.2.cloned.1.call-update) | async-done | bytes 196624 | tf_op jit(solution)/shard_map/reduce_scatter | solution.py:36
  942.4 0.0 copy-done.3
  942.4 2.2 fusion.8
Async XLA Ops:
  6.5 904.2 %copy-start = (bf16[96,4096]{1,0:T(8,128)(2,1)S(1)}, bf16[96,4096]{1,0:T(8,128)(2,1)}, u32[]{:S(2)}) copy-start(bf16[96,4096]{1,0:T(8,128)(2,1)} %param.11) | copy-start | bytes 2359300
  37.7 781.7 %all-to-all-start = ((bf16[64,512,512]{2,0,1:T(8,128)(2,1)}), bf16[64,512,512]{2,0,1:T(8,128)(2,1)}, u32[]{:S(2)}, u32[]{:S(2)}) async-start(bf16[64,512,512]{2,0,1:T(8,128)(2,1)} %copy.24), calls=%async_computation | async-start | bytes 67108864 | tf_op jit(solution)/shard_map/all_to_all | solution.py:35
  45.0 842.7 %all-gather.2.cloned.1.call-start = ((), (), s32[]{:S(2)}) async-start(), calls=%async_computation.3 | async-start | bytes 4718592 | tf_op jit(solution)/shard_map/all_gather | solution.py:29
  45.7 896.7 %reduce-scatter.2.cloned.1.call-start = ((), (), s32[]{:S(2)}) async-start(), calls=%async_computation.2 | async-start | bytes 1769472 | tf_op jit(solution)/shard_map/reduce_scatter | solution.py:36
  842.3 35.3 %copy-start.5 = (bf16[64]{0:T(256)(128)(2,1)S(1)}, bf16[64]{0:T(256)(128)(2,1)}, u32[]{:S(2)}) copy-start(bf16[64]{0:T(256)(128)(2,1)} %param.15) | copy-start | bytes 388
  887.7 6.5 copy-start.4
  894.2 3.8 copy-start.1
  905.9 4.9 copy-start.2
  905.9 36.5 %copy-start.3 = (bf16[512,512]{1,0:T(8,128)(2,1)S(1)}, bf16[512,512]{1,0:T(8,128)(2,1)}, u32[]{:S(2)}) copy-start(bf16[512,512]{1,0:T(8,128)(2,1)} %param.14) | copy-start | bytes 1572868
Sparse Core Ops, SparseCore 0:
  47.9 610.2 all-gather.1
  877.7 64.6 reduce-scatter.1
where the time goes:
time: 952 us; the launch traced here: 951 us
  waiting for transfers between devices  804 us (84%)
  local copies, waits for them, and re-layouts  65.4 us (7%)
  matrix products  60.7 us (6%)
  between operations  13.5 us (1%)
    all_to_all x1, waiting for transfers between devices, on_device(): lax.all_to_all(w_vvv, 'virt', split_axis=1, concat_axis=0, tiled=True)  773 us
    dot_general x1, matrix products, on_device(): jnp.einsum('bep,eba->pa', tau, weights, preferred_element_type=jnp.float32)  35.2 us
    unnamed x13, local copies, waits for them, and re-layouts  31.2 us
    reduce_scatter x1, waiting for transfers between devices, on_device(): lax.psum_scatter(jnp.einsum('bep,eba->pa', tau, weights, preferred_elemen...  30.1 us
    all_to_all x1, local copies, waits for them, and re-layouts, on_device(): lax.all_to_all(w_vvv, 'virt', split_axis=1, concat_axis=0, tiled=True)  22.9 us
  transfers between devices with their start and end apart: 3, of which 2 were waited for; matrix products, arithmetic and copies ran while one was open for 10% of the time, Pallas kernels for 0%

commit v1 on v0

v1 whole, which is shorter than its diff:
```python
import functools

import jax
import jax.numpy as jnp
import numpy as np
from jax import lax
from jax.experimental import pallas as pl
from jax.experimental.pallas import tpu as pltpu
from jax.sharding import PartitionSpec as P


PHASES = (((0, 6), (0, 4, 8, 12, 16)), ((6, 8), (0, 8, 12, 16)))


def chunks_of(columns, rows):
    found = []
    for (a0, a1), cuts in PHASES:
        cuts = sorted({c * rows // 16 for c in cuts})
        for f0, f1 in zip(cuts, cuts[1:]):
            found.append((a0 * columns // 8, a1 * columns // 8, f0, f1))
    return found


def swap(value, axis, size, bit):
    return lax.ppermute(value, axis, [(k, k ^ bit) for k in range(size)])


def spread(piece, size):
    held = {0: piece}
    bit = size // 2
    while bit:
        for key, part in list(held.items()):
            held[key ^ bit] = swap(part, "root", size, bit)
        bit //= 2
    return held


def scatter_sum(partial, size):
    place = lax.axis_index("virt")
    bit = 1
    while bit < size:
        parts = partial.reshape(partial.shape[0] // 2, 2, *partial.shape[1:])
        mine = (place // bit) % 2
        keep = lax.dynamic_index_in_dim(parts, mine, 1, keepdims=False)
        give = lax.dynamic_index_in_dim(parts, 1 - mine, 1, keepdims=False)
        partial = keep + swap(give, "virt", size, bit)
        bit *= 2
    return partial[0]


def pack_body(place_ref, select_ref, slab_ref, *out_refs, chunks):
    rows, span, columns = slab_ref.shape
    group = select_ref.shape[0] // span
    for g in range(0, rows, group):
        part = slab_ref[g : g + group].reshape(group * span, columns)
        moved = jnp.dot(select_ref[...], part, preferred_element_type=jnp.float32)
        moved = moved.astype(jnp.bfloat16).reshape(span, group, columns)
        for (a0, a1, f0, f1), out_ref in zip(chunks, out_refs):
            out_ref[0, :, g : g + group, :] = moved[f0:f1, :, a0:a1]


def pack(w_vvv, virts, roots, root, chunks):
    rows, total, columns = w_vvv.shape
    span = total // (virts * roots)
    group = 16
    if span % 16 or rows % group or any((a1 - a0) % 128 for a0, a1, _, _ in chunks):
        slab = w_vvv.reshape(rows, virts, roots, span, columns)
        slab = lax.dynamic_index_in_dim(slab, root, 2, keepdims=False).transpose(1, 2, 0, 3)
        return [slab[:, f0:f1, :, a0:a1] for a0, a1, f0, f1 in chunks]
    to = np.arange(span * group)[:, None]
    select = np.arange(span * group)[None] == to % group * span + to // group
    shapes = [(virts, f1 - f0, rows, a1 - a0) for a0, a1, f0, f1 in chunks]
    return pl.pallas_call(
        functools.partial(pack_body, chunks=chunks),
        grid_spec=pltpu.PrefetchScalarGridSpec(
            num_scalar_prefetch=1,
            grid=(virts,),
            in_specs=[
                pl.BlockSpec(select.shape, lambda i, q: (0, 0)),
                pl.BlockSpec((rows, span, columns), lambda i, q: (0, i * roots + q[0], 0)),
            ],
            out_specs=[pl.BlockSpec((1, *shape[1:]), lambda i, q: (i, 0, 0, 0)) for shape in shapes],
        ),
        out_shape=[jax.ShapeDtypeStruct(shape, w_vvv.dtype) for shape in shapes],
        cost_estimate=pl.CostEstimate(
            flops=2 * virts * span * rows * columns * span * group,
            bytes_accessed=4 * virts * rows * span * columns,
            transcendentals=0,
        ),
    )(root[None].astype(jnp.int32), jnp.asarray(select, w_vvv.dtype), w_vvv)


def ladder_body(place_ref, tau_ref, *refs, steps, count):
    pieces, out_ref = refs[:count], refs[-1]
    at = pl.program_id(0)

    @pl.when(at == 0)
    def _():
        out_ref[...] = refs[count][...] if len(refs) > count + 1 else jnp.zeros_like(out_ref)

    for k, piece_ref in enumerate(pieces):

        @pl.when(at // steps == k)
        def _(piece_ref=piece_ref):
            sources, taken, rows, columns = piece_ref.shape
            left = [piece_ref[:, f].reshape(sources * rows, columns) for f in range(taken)]
            left = jnp.concatenate(left, 0)
            right = tau_ref[...].reshape(left.shape[0], tau_ref.shape[-1])
            out_ref[...] += lax.dot_general(
                left, right, (((0,), (0,)), ((), ())), preferred_element_type=jnp.float32
            )


def ladder(tau, pieces, running, places, first, roots):
    sources, taken, rows, columns = pieces[0].shape
    total, pairs = tau.shape[1:]
    span = tau.shape[0] // roots
    count = len(pieces)
    step = 4
    while taken % step or first % step or span % step:
        step //= 2
    steps = taken // step
    whole = pl.BlockSpec((columns, pairs), lambda i, q: (0, 0))
    given = () if running is None else (running,)

    def piece_spec(k):
        return pl.BlockSpec(
            (sources, step, rows, columns),
            lambda i, q: (0, jnp.clip(i - k * steps, 0, steps - 1), 0, 0),
        )

    return pl.pallas_call(
        functools.partial(ladder_body, steps=steps, count=count),
        grid_spec=pltpu.PrefetchScalarGridSpec(
            num_scalar_prefetch=1,
            grid=(count * steps,),
            in_specs=[
                pl.BlockSpec(
                    (step, total, pairs),
                    lambda i, q: ((q[i // steps] * span + first) // step + i % steps, 0, 0),
                ),
                *[piece_spec(k) for k in range(count)],
                *[whole for _ in given],
            ],
            out_specs=whole,
        ),
        out_shape=jax.ShapeDtypeStruct((columns, pairs), jnp.float32),
        input_output_aliases={2 + count: 0} if given else {},
        cost_estimate=pl.CostEstimate(
            flops=2 * count * sources * taken * rows * columns * pairs,
            bytes_accessed=2 * count * sources * taken * rows * (columns + pairs),
            transcendentals=0,
        ),
    )(jnp.stack(places).astype(jnp.int32), tau, *pieces, *given)


def on_device(sizes, r2, tau, w_vvv, w_oooo, w_ovoo, fock_oo, fock_vv, r1):
    roots, virts = sizes["root"], sizes["virt"]
    root, virt = lax.axis_index("root"), lax.axis_index("virt")
    f32 = jnp.float32
    block, _, columns = w_vvv.shape
    fblock, _, pairs = tau.shape
    occupied = fock_oo.shape[0]
    pair_rows = w_oooo.shape[0]
    rq = pair_rows // roots

    chunks = chunks_of(columns, fblock // roots)
    sends = pack(w_vvv, virts, roots, root, chunks)
    arrived = []
    for send in sends:
        arrived.append(lax.all_to_all(send, "virt", 0, 0, tiled=True))

    own_rows = lax.dynamic_slice_in_dim(w_oooo, root * rq, rq, 0)
    small = jnp.concatenate([r2, own_rows], 0)
    inner = small.shape[1] // virts
    small = small.reshape(block + rq, virts, inner).transpose(1, 0, 2)
    r2_part = jnp.zeros((virts, block, inner), r2.dtype)
    rows_part = jnp.zeros((virts, rq, inner), r2.dtype)
    for key in range(virts):
        piece = lax.dynamic_index_in_dim(small, virt ^ key, 0)
        if key:
            piece = lax.ppermute(piece, "virt", [(k, k ^ key) for k in range(virts)])
        r2_part = lax.dynamic_update_slice(r2_part, piece[:, :block], (virt ^ key, 0, 0))
        rows_part = lax.dynamic_update_slice(rows_part, piece[:, block:], (virt ^ key, 0, 0))
    r2_part = r2_part.reshape(columns, inner)
    rows_of = spread(rows_part, roots)
    oooo_part = jnp.zeros((virts, roots, rq, inner), r2.dtype)
    for key, part in rows_of.items():
        oooo_part = lax.dynamic_update_slice(oooo_part, part[:, None], (0, root ^ key, 0, 0))
    oooo_part = oooo_part.reshape(pairs, inner)

    window = r2[:, :pairs]
    fock_cols = lax.dynamic_slice_in_dim(fock_vv, virt * block, block, 1)
    extra = jnp.einsum("ep,ae->pa", window, fock_cols, preferred_element_type=f32)
    outer = pairs // occupied
    cube = r2.reshape(block, occupied, occupied)
    first = jnp.einsum("mi,amj->aij", fock_oo[:, :outer], cube, preferred_element_type=f32)
    second = jnp.einsum("mj,aim->aij", fock_oo, cube[:, :outer], preferred_element_type=f32)
    occ = (first + second).reshape(block, pairs).T
    placed = lax.dynamic_update_slice(jnp.zeros((pairs, columns), f32), occ, (0, virt * block))
    extra = extra - placed
    extra = extra + jnp.einsum("pk,ak->pa", oooo_part, r2_part, preferred_element_type=f32)

    singles = jnp.dot(
        r1[None, :], w_ovoo.reshape(w_ovoo.shape[0], -1), preferred_element_type=f32
    ).reshape(pair_rows, -1)

    running = {}
    results = {}
    for index, (a0, a1, f0, f1) in enumerate(chunks):
        held = spread(arrived[index], roots)
        for keys in groups_of(index, len(chunks), roots):
            running[a0] = ladder(
                tau, [held[k] for k in keys], running.get(a0), [root ^ k for k in keys], f0, roots
            )
        if f1 == fblock // roots:
            partial = running[a0].T + extra[:, a0:a1]
            summed = scatter_sum(partial.reshape(virts, pair_rows, a1 - a0), virts)
            results[a0] = summed - singles[:, a0:a1]
    return jnp.concatenate([results[a0] for a0 in sorted(results)], 1)


def groups_of(index, count, roots):
    keys = list(range(roots))
    if index + 4 < count:
        return [keys]
    return [keys[: roots // 2], keys[roots // 2 :]]


def solution(mesh):
    sizes = dict(mesh.shape)
    in_specs = (
        P("virt", "root"),
        P("virt", None, "root"),
        P("virt", None, None),
        P("virt", None),
        P(None, "virt", None),
        P(),
        P(),
        P("root"),
    )
    out_specs = P(("root", "virt"), None)

    def body(*args):
        return on_device(sizes, *args)

    return jax.shard_map(
        body, mesh=mesh, in_specs=in_specs, out_specs=out_specs, check_vma=False
    )
```

time: 952 us -> 506 us (0.53)
  waiting for transfers between devices: 804 us -> 182 us
  blocking collectives: 0 us -> 109 us
  Pallas kernels: 0 us -> 101 us
  matrix products: 60.7 us -> 17.1 us
  starting transfers between devices: 7.56 us -> 50.7 us
  local copies, waits for them, and re-layouts: 65.4 us -> 31.9 us
  between operations: 13.5 us -> 0.88 us
    all_to_all x1 -> x3, waiting for transfers between devices: 773 us -> 36.1 us  [on_device(): arrived.append(lax.all_to_all(send, 'virt', 0, 0, tiled=True))]
    ppermute x0 -> x37, waiting for transfers between devices: none -> 146 us  [the longest x30 130 us: swap(): return lax.ppermute(value, axis, [(k, k ^ bit) for k in range(size)])]
    all_to_all x0 -> x4, blocking collectives: none -> 109 us  [on_device(): arrived.append(lax.all_to_all(send, 'virt', 0, 0, tiled=True))]
    pallas_call x0 -> x12, Pallas kernels: none -> 101 us  [the longest x11 90.5 us: ladder(): pl.pallas_call(functools.partial(ladder_body, steps=steps, count=count),...]
    dot_general x5 -> x4, matrix products: 50.5 us -> 7.64 us  [the longest x1 3.8 us: on_device(): jnp.einsum('pk,ak->pa', oooo_part, r2_part, preferred_element_type=f32)]
    ppermute x0 -> x37, starting transfers between devices: none -> 38.1 us  [the longest x30 22.6 us: swap(): return lax.ppermute(value, axis, [(k, k ^ bit) for k in range(size)])]
    reduce_scatter x1 -> x0, waiting for transfers between devices: 30.1 us -> none  [on_device(): lax.psum_scatter(jnp.einsum('bep,eba->pa', tau, weights, preferred_elemen...]
    unnamed x13 -> x67, local copies, waits for them, and re-layouts: 31.2 us -> 4.9 us
  transfers between devices with their start and end apart: 3 -> 40, of which waited for: 2 -> 14; matrix products, arithmetic and copies ran while one was open for 10% -> 11% of each run, Pallas kernels for 0% -> 18%
where the time goes in v1:
time: 506 us; the launch traced here: 499 us
  waiting for transfers between devices  182 us (36%)
  blocking collectives  109 us (22%)
  Pallas kernels  101 us (20%)
  starting transfers between devices  50.7 us (10%)
  local copies, waits for them, and re-layouts  31.9 us (6%)
  matrix products  17.1 us (3%)
  other arithmetic  6.4 us (1%)
    ppermute x30, waiting for transfers between devices, swap(): return lax.ppermute(value, axis, [(k, k ^ bit) for k in range(size)])  130 us
    all_to_all x4, blocking collectives, on_device(): arrived.append(lax.all_to_all(send, 'virt', 0, 0, tiled=True))  109 us
    pallas_call x11, Pallas kernels, ladder(): pl.pallas_call(functools.partial(ladder_body, steps=steps, count=count),...  90.5 us
    all_to_all x3, waiting for transfers between devices, on_device(): arrived.append(lax.all_to_all(send, 'virt', 0, 0, tiled=True))  36.1 us
    ppermute x30, starting transfers between devices, swap(): return lax.ppermute(value, axis, [(k, k ^ bit) for k in range(size)])  22.6 us
    ppermute x7, waiting for transfers between devices, on_device(): piece = lax.ppermute(piece, 'virt', [(k, k ^ key) for k in range(virts)])  16.1 us
    ppermute x7, starting transfers between devices, on_device(): piece = lax.ppermute(piece, 'virt', [(k, k ^ key) for k in range(virts)])  15.6 us
    all_to_all x3, starting transfers between devices, on_device(): arrived.append(lax.all_to_all(send, 'virt', 0, 0, tiled=True))  12.6 us
  transfers between devices with their start and end apart: 40, of which 14 were waited for; matrix products, arithmetic and copies ran while one was open for 11% of the time, Pallas kernels for 18%

profile of v1, /device:TPU:0, one launch (start us, length us, event | category | flops | bytes accessed | tf_op | source)
XLA Modules:
  0.0 498.9 jit_solution(2095698959669316094)
XLA Ops:
  0.0 10.3 %shard_map.91 = (bf16[8,4,64,384]{3,2,1,0:T(8,128)(2,1)}, bf16[8,4,64,384]{3,2,1,0:T(8,128)(2,1)}, bf16[8,4,64,384]{3,2,1,0:T(8,128)(2,1)}, bf16[8,4,64,384]{3,2...) custom-call(s32[1]{0:T(128)} %bitcast.2.place_ref, ...), custom_call_target="tpu_custom_call" | custom-call | flops 2147483648 | bytes 16777216 | tf_op jit(solution)/shard_map/pallas_call | solution.py:73
  10.3 22.1 %all_to_all.35.refs_0_ = bf16[8,4,64,128]{3,2,1,0:T(8,128)(2,1)} all-to-all(bf16[8,4,64,128]{3,2,1,0:T(8,128)(2,1)} %get-tuple-element.17), channel_id=1, replica_groups=mesh['root'=4,'virt'=8] {'virt'}, dimensions={0} | all-to-all | bytes 1048576 | tf_op jit(solution)/shard_map/all_to_all | solution.py:171
  32.4 18.0 %all_to_all.36.refs_0_ = bf16[8,4,64,128]{3,2,1,0:T(8,128)(2,1)} all-to-all(bf16[8,4,64,128]{3,2,1,0:T(8,128)(2,1)} %get-tuple-element.16), channel_id=1, replica_groups=mesh['root'=4,'virt'=8] {'virt'}, dimensions={0} | all-to-all | bytes 1048576 | tf_op jit(solution)/shard_map/all_to_all | solution.py:171
  50.4 28.8 %all_to_all.37.refs_0_ = bf16[8,8,64,128]{3,2,1,0:T(8,128)(2,1)S(1)} all-to-all(bf16[8,8,64,128]{3,2,1,0:T(8,128)(2,1)S(1)} %copy-done.13), channel_id=1, replica_groups=mesh['root'=4,'virt'=8] {'virt'}, dimensions={0} | all-to-all | bytes 2097152 | tf_op jit(solution)/shard_map/all_to_all | solution.py:171
  79.2 40.1 %all_to_all.38.refs_0_ = bf16[8,4,64,384]{3,2,1,0:T(8,128)(2,1)} all-to-all(bf16[8,4,64,384]{3,2,1,0:T(8,128)(2,1)S(1)} %copy-done.9), channel_id=1, replica_groups=mesh['root'=4,'virt'=8] {'virt'}, dimensions={0} | all-to-all | bytes 3145728 | tf_op jit(solution)/shard_map/all_to_all | solution.py:171
  119.3 4.3 all-to-all-start.2
  123.6 36.1 %all-to-all-done.2.refs_0_ = bf16[8,4,64,384]{3,2,1,0:T(8,128)(2,1)} async-done(((bf16[8,4,64,384]{3,2,1,0:T(8,128)(2,1)}), bf16[8,4,64,384]{3,2,1,0:T(8,128)(2,1)}, u32[]{:S(2)}, u32[]{:S(2)}) %all-to-all-start.2) | async-done | bytes 1572896 | tf_op jit(solution)/shard_map/all_to_all | solution.py:171
  159.7 4.4 all-to-all-start.1
  192.9 4.5 collective-permute-start.18
  198.9 13.3 %collective-permute-done.15 = bf16[1,88,512]{2,1,0:T(8,128)(2,1)} collective-permute-done((bf16[1,88,512]{2,1,0:T(8,128)(2,1)}, bf16[1,88,512]{2,1,0:T(8,128)(2,1)}, u32[]{:S(2)}, u32[]{:S(2)}) %collective-permute-start.15) | collective-permute-done | bytes 90144 | tf_op jit(solution)/shard_map/ppermute | solution.py:182
  214.9 3.9 all-to-all-start
  224.1 25.8 %collective-permute-done.19 = bf16[8,24,512]{2,1,0:T(8,128)(2,1)S(1)} collective-permute-done((bf16[8,24,512]{2,1,0:T(8,128)(2,1)S(1)}, bf16[8,24,512]{2,1,0:T(8,128)(2,1)S(1)}, u32[]{:S(2)}, u32[]{:S(2)}) %collective-permute-start.19) | collective-permute-done | bytes 196640 | tf_op jit(solution)/shard_map/ppermute | solution.py:25
  254.1 7.0 %collective-permute-done.28.refs_0_ = bf16[8,4,64,128]{3,2,1,0:T(8,128)(2,1)S(1)} collective-permute-done((bf16[8,4,64,128]{3,2,1,0:T(8,128)(2,1)}, bf16[8,4,64,128]{3,2,1,0:T(8,128)(2,1)S(1)}, u32[]{:S(2)}, u32[]{:S(2)}) %collective-permute-start.28) | collective-permute-done | bytes 524320 | tf_op jit(solution)/shard_map/ppermute | solution.py:25
  262.6 6.7 %collective-permute-done.25.refs_0_ = bf16[8,4,64,128]{3,2,1,0:T(8,128)(2,1)S(1)} collective-permute-done((bf16[8,4,64,128]{3,2,1,0:T(8,128)(2,1)S(1)}, bf16[8,4,64,128]{3,2,1,0:T(8,128)(2,1)S(1)}, u32[]{:S(2)}, u32[]{:S(2)}) %collective-permute-start.25) | collective-permute-done | bytes 524320 | tf_op jit(solution)/shard_map/ppermute | solution.py:25
  283.9 23.1 %collective-permute-done.10.refs_2_ = bf16[8,4,64,384]{3,2,1,0:T(8,128)(2,1)} collective-permute-done((bf16[8,4,64,384]{3,2,1,0:T(8,128)(2,1)}, bf16[8,4,64,384]{3,2,1,0:T(8,128)(2,1)}, u32[]{:S(2)}, u32[]{:S(2)}) %collective-permute-start.10) | collective-permute-done | bytes 1572896 | tf_op jit(solution)/shard_map/ppermute | solution.py:25
  311.5 29.3 %collective-permute-done.7.refs_2_ = bf16[8,4,64,384]{3,2,1,0:T(8,128)(2,1)} collective-permute-done((bf16[8,4,64,384]{3,2,1,0:T(8,128)(2,1)}, bf16[8,4,64,384]{3,2,1,0:T(8,128)(2,1)}, u32[]{:S(2)}, u32[]{:S(2)}) %collective-permute-start.7) | collective-permute-done | bytes 1572896 | tf_op jit(solution)/shard_map/ppermute | solution.py:25
  344.5 8.1 %shard_map.97.refs_2_ = f32[128,768]{1,0:T(8,128)} custom-call(s32[2]{0:T(128)} %pad_add_fusion.1.place_ref, bf16[64,512,768]{2,1,0:T(8,128)(2,1)} %tau_ref.21, bf16[8,8,64,128]{3,2,1,0:T(8,128)(2,1)} %copy-done.5, bf16[8,8,64,128]{3,2,1,0:T(8,128)(2,1)} %copy-done.11), custom_call_target="tpu_custom_call" | custom-call | flops 1610612736 | bytes 14680064 | tf_op jit(solution)/shard_map/pallas_call | solution.py:132
  352.7 8.3 %shard_map.98.refs_2_ = f32[128,768]{1,0:T(8,128)} custom-call(s32[2]{0:T(128)} %pad_add_fusion.place_ref, bf16[64,512,768]{2,1,0:T(8,128)(2,1)} %tau_ref.21, bf16[8,8,64,128]{3,2,1,0:T(8,128)(2,1)} %copy-done.10, bf16[8,8,64,128]{3,2,1,0:T(8,128)(2,1)} %copy-done.12, f32[128,768]{1,0:T(8,128)} %shard_map.97.refs_2_), custom_call_target="tpu_custom_call", output_to_operand_aliasing={{}: (4, {})} | custom-call | flops 1610612736 | bytes 14680064 | tf_op jit(solution)/shard_map/pallas_call | solution.py:132
  361.5 13.0 %collective-permute-done.4.refs_2_ = bf16[8,4,64,384]{3,2,1,0:T(8,128)(2,1)} collective-permute-done((bf16[8,4,64,384]{3,2,1,0:T(8,128)(2,1)}, bf16[8,4,64,384]{3,2,1,0:T(8,128)(2,1)}, u32[]{:S(2)}, u32[]{:S(2)}) %collective-permute-start.4) | collective-permute-done | bytes 1572896 | tf_op jit(solution)/shard_map/ppermute | solution.py:25
  374.4 5.4 %shard_map.99.refs_2_ = f32[128,768]{1,0:T(8,128)} custom-call(s32[2]{0:T(128)} %pad_add_fusion.1.place_ref, bf16[64,512,768]{2,1,0:T(8,128)(2,1)} %tau_ref.21, bf16[8,4,64,128]{3,2,1,0:T(8,128)(2,1)} %all_to_all.35.refs_0_, bf16[8,4,64,128]{3,2,1,0:T(8,128)(2,1)} %copy-done.21, f32[128,768]{1,0:T(8,128)} %shard_map.98.refs_2_), custom_call_target="tpu_custom_call", output_to_operand_aliasing={{}: (4, {})} | custom-call | flops 805306368 | bytes 7340032 | tf_op jit(solution)/shard_map/pallas_call | solution.py:132
  379.8 5.4 %shard_map.100.refs_2_ = f32[128,768]{1,0:T(8,128)} custom-call(s32[2]{0:T(128)} %pad_add_fusion.place_ref, bf16[64,512,768]{2,1,0:T(8,128)(2,1)} %tau_ref.21, bf16[8,4,64,128]{3,2,1,0:T(8,128)(2,1)} %copy-done.19, bf16[8,4,64,128]{3,2,1,0:T(8,128)(2,1)} %copy-done.22, f32[128,768]{1,0:T(8,128)} %shard_map.99.refs_2_), custom_call_target="tpu_custom_call", output_to_operand_aliasing={{}: (4, {})} | custom-call | flops 805306368 | bytes 7340032 | tf_op jit(solution)/shard_map/pallas_call | solution.py:132
  385.2 5.4 %shard_map.101.refs_2_ = f32[128,768]{1,0:T(8,128)} custom-call(s32[2]{0:T(128)} %pad_add_fusion.1.place_ref, bf16[64,512,768]{2,1,0:T(8,128)(2,1)} %tau_ref.21, bf16[8,4,64,128]{3,2,1,0:T(8,128)(2,1)} %all_to_all.36.refs_0_, bf16[8,4,64,128]{3,2,1,0:T(8,128)(2,1)} %collective-permute-done.27.refs_1_, ...), custom_call_target="tpu_custom_call", output_to_operand_aliasing={{}: (4, {})} | custom-call | flops 805306368 | bytes 7340032 | tf_op jit(solution)/shard_map/pallas_call | solution.py:132
  390.5 5.4 %shard_map.102 = f32[128,768]{1,0:T(8,128)} custom-call(s32[2]{0:T(128)} %pad_add_fusion.place_ref, bf16[64,512,768]{2,1,0:T(8,128)(2,1)} %tau_ref.21, bf16[8,4,64,128]{3,2,1,0:T(8,128)(2,1)} %copy-done.20, bf16[8,4,64,128]{3,2,1,0:T(8,128)(2,1)} %copy-done.23, f32[128,768]{1,0:T(8,128)} %shard_map.101.refs_2_), custom_call_target="tpu_custom_call", output_to_operand_aliasing={{}: (4, {})} | custom-call | flops 805306368 | bytes 7340032 | tf_op jit(solution)/shard_map/pallas_call | solution.py:132
  395.9 11.7 %collective-permute-done.refs_0_ = bf16[8,4,64,384]{3,2,1,0:T(8,128)(2,1)} collective-permute-done((bf16[8,4,64,384]{3,2,1,0:T(8,128)(2,1)S(1)}, bf16[8,4,64,384]{3,2,1,0:T(8,128)(2,1)}, u32[]{:S(2)}, u32[]{:S(2)}) %collective-permute-start) | collective-permute-done | bytes 1572896 | tf_op jit(solution)/shard_map/ppermute | solution.py:25
  409.6 12.4 %shard_map.92.refs_4_ = f32[384,768]{1,0:T(8,128)} custom-call(s32[4]{0:T(128)} %pad_add_fusion.2.place_ref, bf16[64,512,768]{2,1,0:T(8,128)(2,1)} %tau_ref.21, bf16[8,4,64,384]{3,2,1,0:T(8,128)(2,1)} %all_to_all.38.refs_0_, bf16[8,4,64,384]{3,2,1,0:T(8,128)(2,1)} %collective-permute-done.9.refs_1_, bf16[8,4,64,384]{3,2,1,0:T(8,128)(2,1)} %collective-permute-done.10.refs_2_, ...), custom_call_target="tpu_custom_call" | custom-call | flops 4831838208 | bytes 18874368 | tf_op jit(solution)/shard_map/pallas_call | solution.py:132
  423.7 12.1 %shard_map.93.refs_4_ = f32[384,768]{1,0:T(8,128)} custom-call(s32[4]{0:T(128)} %pad_add_fusion.2.place_ref, bf16[64,512,768]{2,1,0:T(8,128)(2,1)} %tau_ref.21, bf16[8,4,64,384]{3,2,1,0:T(8,128)(2,1)} %all-to-all-done.2.refs_0_, bf16[8,4,64,384]{3,2,1,0:T(8,128)(2,1)} %collective-permute-done.6.refs_1_, ...), custom_call_target="tpu_custom_call", output_to_operand_aliasing={{}: (6, {})} | custom-call | flops 4831838208 | bytes 18874368 | tf_op jit(solution)/shard_map/pallas_call | solution.py:132
  435.8 12.3 %shard_map.94.refs_2_ = f32[384,768]{1,0:T(8,128)} custom-call(s32[4]{0:T(128)} %pad_add_fusion.2.place_ref, bf16[64,512,768]{2,1,0:T(8,128)(2,1)} %tau_ref.21, bf16[8,4,64,384]{3,2,1,0:T(8,128)(2,1)} %all-to-all-done.1.refs_0_, bf16[8,4,64,384]{3,2,1,0:T(8,128)(2,1)} %collective-permute-done.3.refs_1_, ...), custom_call_target="tpu_custom_call", output_to_operand_aliasing={{}: (6, {})} | custom-call | flops 4831838208 | bytes 18874368 | tf_op jit(solution)/shard_map/pallas_call | solution.py:132
  448.1 7.7 %shard_map.95.refs_2_ = f32[384,768]{1,0:T(8,128)} custom-call(s32[2]{0:T(128)} %pad_add_fusion.1.place_ref, bf16[64,512,768]{2,1,0:T(8,128)(2,1)} %tau_ref.21, bf16[8,4,64,384]{3,2,1,0:T(8,128)(2,1)} %copy-done.2, bf16[8,4,64,384]{3,2,1,0:T(8,128)(2,1)} %collective-permute-done.2.refs_1_, f32[384,768]{1,0:T(8,128)} %shard_map.94.refs_2_), custom_call_target="tpu_custom_call", output_to_operand_aliasing={{}: (4, {})} | custom-call | flops 2415919104 | bytes 9437184 | tf_op jit(solution)/shard_map/pallas_call | solution.py:132
  455.9 8.0 %shard_map.96 = f32[384,768]{1,0:T(8,128)} custom-call(s32[2]{0:T(128)} %pad_add_fusion.place_ref, bf16[64,512,768]{2,1,0:T(8,128)(2,1)} %tau_ref.21, bf16[8,4,64,384]{3,2,1,0:T(8,128)(2,1)} %collective-permute-done.refs_0_, bf16[8,4,64,384]{3,2,1,0:T(8,128)(2,1)} %collective-permute-done.1.refs_1_, ...), custom_call_target="tpu_custom_call", output_to_operand_aliasing={{}: (4, {})} | custom-call | flops 2415919104 | bytes 9437184 | tf_op jit(solution)/shard_map/pallas_call | solution.py:132
  466.1 9.5 %fusion = f32[1,96,512]{2,0,1:T(1,128)S(1)} fusion(bf16[64]{0:T(256)(128)(2,1)S(1)} %copy-done.28, bf16[8,8,96,512]{3,2,1,0:T(8,128)(2,1)} %bitcast.126), kind=kOutput, calls=%fused_computation | convolution fusion | flops 6291456 | bytes 6488192 | tf_op jit(solution)/shard_map/dot_general | solution.py:204
  484.9 4.9 collective-permute-done.23
  491.8 6.1 %collective-permute-done.24 = f32[1,96,384]{2,1,0:T(8,128)S(1)} collective-permute-done((f32[1,96,384]{2,1,0:T(8,128)S(1)}, f32[1,96,384]{2,1,0:T(8,128)S(1)}, u32[]{:S(2)}, u32[]{:S(2)}) %collective-permute-start.24) | collective-permute-done | bytes 147488 | tf_op jit(solution)/shard_map/ppermute | solution.py:25
  (188 shorter events, 84.7 us)
Async XLA Ops:
  119.3 40.5 %all-to-all-start.2 = ((bf16[8,4,64,384]{3,2,1,0:T(8,128)(2,1)}), bf16[8,4,64,384]{3,2,1,0:T(8,128)(2,1)}, u32[]{:S(2)}, u32[]{:S(2)}) async-start(bf16[8,4,64,384]{3,2,1,0:T(8,128)(2,1)} %get-tuple-element.14), calls=%async_computation.2 | async-start | bytes 3145728 | tf_op jit(solution)/shard_map/all_to_all | solution.py:171
  159.7 55.1 %all-to-all-start.1 = ((bf16[8,4,64,384]{3,2,1,0:T(8,128)(2,1)}), bf16[8,4,64,384]{3,2,1,0:T(8,128)(2,1)}, u32[]{:S(2)}, u32[]{:S(2)}) async-start(bf16[8,4,64,384]{3,2,1,0:T(8,128)(2,1)} %get-tuple-element.13), calls=%async_computation.1 | async-start | bytes 3145728 | tf_op jit(solution)/shard_map/all_to_all | solution.py:171
  167.4 19.9 %collective-permute-start.12 = (bf16[1,88,512]{2,1,0:T(8,128)(2,1)}, bf16[1,88,512]{2,1,0:T(8,128)(2,1)}, u32[]{:S(2)}, u32[]{:S(2)}) collective-permute-start(bf16[1,88,512]{2,1,0:T(8,128)(2,1)} %bitcast.109), channel_id=1, source_target_pairs={{0,1},{1,0},{2,3},{3,2},{4,5},{5,4},{6,7},{7,6},{8,9},{9,8},{10,11... | collective-permute-start | bytes 270344 | tf_op jit(solution)/shard_map/ppermute | solution.py:182
  169.9 23.0 %collective-permute-start.13 = (bf16[1,88,512]{2,1,0:T(8,128)(2,1)}, bf16[1,88,512]{2,1,0:T(8,128)(2,1)}, u32[]{:S(2)}, u32[]{:S(2)}) collective-permute-start(bf16[1,88,512]{2,1,0:T(8,128)(2,1)} %bitcast.108), channel_id=1, source_target_pairs={{0,2},{1,3},{2,0},{3,1},{4,6},{5,7},{6,4},{7,5},{8,10},{9,11},{10,... | collective-permute-start | bytes 270344 | tf_op jit(solution)/shard_map/ppermute | solution.py:182
  172.0 26.1 %collective-permute-start.14 = (bf16[1,88,512]{2,1,0:T(8,128)(2,1)}, bf16[1,88,512]{2,1,0:T(8,128)(2,1)}, u32[]{:S(2)}, u32[]{:S(2)}) collective-permute-start(bf16[1,88,512]{2,1,0:T(8,128)(2,1)} %bitcast.107), channel_id=1, source_target_pairs={{0,3},{1,2},{2,1},{3,0},{4,7},{5,6},{6,5},{7,4},{8,11},{9,10},{10,... | collective-permute-start | bytes 270344 | tf_op jit(solution)/shard_map/ppermute | solution.py:182
  172.8 39.4 %collective-permute-start.15 = (bf16[1,88,512]{2,1,0:T(8,128)(2,1)}, bf16[1,88,512]{2,1,0:T(8,128)(2,1)}, u32[]{:S(2)}, u32[]{:S(2)}) collective-permute-start(bf16[1,88,512]{2,1,0:T(8,128)(2,1)} %bitcast.106), channel_id=1, source_target_pairs={{0,4},{1,5},{2,6},{3,7},{4,0},{5,1},{6,2},{7,3},{8,12},{9,13},{10,... | collective-permute-start | bytes 270344 | tf_op jit(solution)/shard_map/ppermute | solution.py:182
  176.3 37.9 %collective-permute-start.16 = (bf16[1,88,512]{2,1,0:T(8,128)(2,1)}, bf16[1,88,512]{2,1,0:T(8,128)(2,1)}, u32[]{:S(2)}, u32[]{:S(2)}) collective-permute-start(bf16[1,88,512]{2,1,0:T(8,128)(2,1)} %bitcast.105), channel_id=1, source_target_pairs={{0,5},{1,4},{2,7},{3,6},{4,1},{5,0},{6,3},{7,2},{8,13},{9,12},{10,... | collective-permute-start | bytes 270344 | tf_op jit(solution)/shard_map/ppermute | solution.py:182
  187.3 31.5 %collective-permute-start.17 = (bf16[1,88,512]{2,1,0:T(8,128)(2,1)}, bf16[1,88,512]{2,1,0:T(8,128)(2,1)}, u32[]{:S(2)}, u32[]{:S(2)}) collective-permute-start(bf16[1,88,512]{2,1,0:T(8,128)(2,1)} %bitcast.104), channel_id=1, source_target_pairs={{0,6},{1,7},{2,4},{3,5},{4,2},{5,3},{6,0},{7,1},{8,14},{9,15},{10,... | collective-permute-start | bytes 270344 | tf_op jit(solution)/shard_map/ppermute | solution.py:182
  192.9 28.2 %collective-permute-start.18 = (bf16[1,88,512]{2,1,0:T(8,128)(2,1)}, bf16[1,88,512]{2,1,0:T(8,128)(2,1)}, u32[]{:S(2)}, u32[]{:S(2)}) collective-permute-start(bf16[1,88,512]{2,1,0:T(8,128)(2,1)} %bitcast.103), channel_id=1, source_target_pairs={{0,7},{1,6},{2,5},{3,4},{4,3},{5,2},{6,1},{7,0},{8,15},{9,14},{10,... | collective-permute-start | bytes 270344 | tf_op jit(solution)/shard_map/ppermute | solution.py:182
  214.9 69.1 %all-to-all-start = ((bf16[8,4,64,384]{3,2,1,0:T(8,128)(2,1)}), bf16[8,4,64,384]{3,2,1,0:T(8,128)(2,1)S(1)}, u32[]{:S(2)}, u32[]{:S(2)}) async-start(bf16[8,4,64,384]{3,2,1,0:T(8,128)(2,1)} %get-tuple-element.12), calls=%async_computation | async-start | bytes 3145728 | tf_op jit(solution)/shard_map/all_to_all | solution.py:171
  219.6 53.0 %collective-permute-start.31 = (bf16[8,8,64,128]{3,2,1,0:T(8,128)(2,1)S(1)}, bf16[8,8,64,128]{3,2,1,0:T(8,128)(2,1)S(1)}, u32[]{:S(2)}, u32[]{:S(2)}) collective-permute-start(bf16[8,8,64,128]{3,2,1,0:T(8,128)(2,1)S(1)} %all_to_all.37.refs_0_), channel_id=1, source_target_pairs={{0,16},{8,24},{16,0},{24,8},{1,17},{9,25},{17,1},{25,9},{2,18},{10... | collective-permute-start | bytes 3145736 | tf_op jit(solution)/shard_map/ppermute | solution.py:25
  221.9 28.0 %collective-permute-start.19 = (bf16[8,24,512]{2,1,0:T(8,128)(2,1)S(1)}, bf16[8,24,512]{2,1,0:T(8,128)(2,1)S(1)}, u32[]{:S(2)}, u32[]{:S(2)}) collective-permute-start(bf16[8,24,512]{2,1,0:T(8,128)(2,1)S(1)} %slice_dynamic-update-slice_fusion.8), channel_id=1, source_target_pairs={{0,16},{8,24},{16,0},{24,8},{1,17},{9,25},{17,1},{25,9},{2,18},{10... | collective-permute-start | bytes 589832 | tf_op jit(solution)/shard_map/ppermute | solution.py:25
  222.4 28.0 %collective-permute-start.20 = (bf16[8,24,512]{2,1,0:T(8,128)(2,1)S(1)}, bf16[8,24,512]{2,1,0:T(8,128)(2,1)S(1)}, u32[]{:S(2)}, u32[]{:S(2)}) collective-permute-start(bf16[8,24,512]{2,1,0:T(8,128)(2,1)S(1)} %slice_dynamic-update-slice_fusion.8), channel_id=1, source_target_pairs={{0,8},{8,0},{16,24},{24,16},{1,9},{9,1},{17,25},{25,17},{2,10},{10... | collective-permute-start | bytes 589832 | tf_op jit(solution)/shard_map/ppermute | solution.py:25
  222.4 38.7 %collective-permute-start.28 = (bf16[8,4,64,128]{3,2,1,0:T(8,128)(2,1)}, bf16[8,4,64,128]{3,2,1,0:T(8,128)(2,1)S(1)}, u32[]{:S(2)}, u32[]{:S(2)}) collective-permute-start(bf16[8,4,64,128]{3,2,1,0:T(8,128)(2,1)} %all_to_all.35.refs_0_), channel_id=1, source_target_pairs={{0,16},{8,24},{16,0},{24,8},{1,17},{9,25},{17,1},{25,9},{2,18},{10... | collective-permute-start | bytes 1572872 | tf_op jit(solution)/shard_map/ppermute | solution.py:25
  249.9 19.5 %collective-permute-start.30 = (bf16[8,4,64,128]{3,2,1,0:T(8,128)(2,1)S(1)}, bf16[8,4,64,128]{3,2,1,0:T(8,128)(2,1)S(1)}, u32[]{:S(2)}, u32[]{:S(2)}) collective-permute-start(bf16[8,4,64,128]{3,2,1,0:T(8,128)(2,1)S(1)} %copy-done.8), channel_id=1, source_target_pairs={{0,8},{8,0},{16,24},{24,16},{1,9},{9,1},{17,25},{25,17},{2,10},{10... | collective-permute-start | bytes 1572872 | tf_op jit(solution)/shard_map/ppermute | solution.py:25
  250.4 18.9 %collective-permute-start.25 = (bf16[8,4,64,128]{3,2,1,0:T(8,128)(2,1)S(1)}, bf16[8,4,64,128]{3,2,1,0:T(8,128)(2,1)S(1)}, u32[]{:S(2)}, u32[]{:S(2)}) collective-permute-start(bf16[8,4,64,128]{3,2,1,0:T(8,128)(2,1)S(1)} %copy-done.7), channel_id=1, source_target_pairs={{0,16},{8,24},{16,0},{24,8},{1,17},{9,25},{17,1},{25,9},{2,18},{10... | collective-permute-start | bytes 1572872 | tf_op jit(solution)/shard_map/ppermute | solution.py:25
  253.4 19.0 %collective-permute-start.27 = (bf16[8,4,64,128]{3,2,1,0:T(8,128)(2,1)S(1)}, bf16[8,4,64,128]{3,2,1,0:T(8,128)(2,1)}, u32[]{:S(2)}, u32[]{:S(2)}) collective-permute-start(bf16[8,4,64,128]{3,2,1,0:T(8,128)(2,1)S(1)} %copy-done.7), channel_id=1, source_target_pairs={{0,8},{8,0},{16,24},{24,16},{1,9},{9,1},{17,25},{25,17},{2,10},{10... | collective-permute-start | bytes 1572872 | tf_op jit(solution)/shard_map/ppermute | solution.py:25
  261.1 13.4 %collective-permute-start.29 = (bf16[8,4,64,128]{3,2,1,0:T(8,128)(2,1)S(1)}, bf16[8,4,64,128]{3,2,1,0:T(8,128)(2,1)S(1)}, u32[]{:S(2)}, u32[]{:S(2)}) collective-permute-start(bf16[8,4,64,128]{3,2,1,0:T(8,128)(2,1)S(1)} %collective-permute-done.28.refs_0_), channel_id=1, source_target_pairs={{0,8},{8,0},{16,24},{24,16},{1,9},{9,1},{17,25},{25,17},{2,10},{10... | collective-permute-start | bytes 1572872 | tf_op jit(solution)/shard_map/ppermute | solution.py:25
  269.4 37.7 %collective-permute-start.10 = (bf16[8,4,64,384]{3,2,1,0:T(8,128)(2,1)}, bf16[8,4,64,384]{3,2,1,0:T(8,128)(2,1)}, u32[]{:S(2)}, u32[]{:S(2)}) collective-permute-start(bf16[8,4,64,384]{3,2,1,0:T(8,128)(2,1)} %all_to_all.38.refs_0_), channel_id=1, source_target_pairs={{0,16},{8,24},{16,0},{24,8},{1,17},{9,25},{17,1},{25,9},{2,18},{10... | collective-permute-start | bytes 4718600 | tf_op jit(solution)/shard_map/ppermute | solution.py:25
  274.5 35.9 %collective-permute-start.9 = (bf16[8,4,64,384]{3,2,1,0:T(8,128)(2,1)}, bf16[8,4,64,384]{3,2,1,0:T(8,128)(2,1)}, u32[]{:S(2)}, u32[]{:S(2)}) collective-permute-start(bf16[8,4,64,384]{3,2,1,0:T(8,128)(2,1)} %all_to_all.38.refs_0_), channel_id=1, source_target_pairs={{0,8},{8,0},{16,24},{24,16},{1,9},{9,1},{17,25},{25,17},{2,10},{10... | collective-permute-start | bytes 4718600 | tf_op jit(solution)/shard_map/ppermute | solution.py:25
  276.2 64.5 %collective-permute-start.7 = (bf16[8,4,64,384]{3,2,1,0:T(8,128)(2,1)}, bf16[8,4,64,384]{3,2,1,0:T(8,128)(2,1)}, u32[]{:S(2)}, u32[]{:S(2)}) collective-permute-start(bf16[8,4,64,384]{3,2,1,0:T(8,128)(2,1)} %all-to-all-done.2.refs_0_), channel_id=1, source_target_pairs={{0,16},{8,24},{16,0},{24,8},{1,17},{9,25},{17,1},{25,9},{2,18},{10... | collective-permute-start | bytes 4718600 | tf_op jit(solution)/shard_map/ppermute | solution.py:25
  280.8 80.2 %collective-permute-start.6 = (bf16[8,4,64,384]{3,2,1,0:T(8,128)(2,1)}, bf16[8,4,64,384]{3,2,1,0:T(8,128)(2,1)}, u32[]{:S(2)}, u32[]{:S(2)}) collective-permute-start(bf16[8,4,64,384]{3,2,1,0:T(8,128)(2,1)} %all-to-all-done.2.refs_0_), channel_id=1, source_target_pairs={{0,8},{8,0},{16,24},{24,16},{1,9},{9,1},{17,25},{25,17},{2,10},{10... | collective-permute-start | bytes 4718600 | tf_op jit(solution)/shard_map/ppermute | solution.py:25
  280.9 93.6 %collective-permute-start.4 = (bf16[8,4,64,384]{3,2,1,0:T(8,128)(2,1)}, bf16[8,4,64,384]{3,2,1,0:T(8,128)(2,1)}, u32[]{:S(2)}, u32[]{:S(2)}) collective-permute-start(bf16[8,4,64,384]{3,2,1,0:T(8,128)(2,1)} %all-to-all-done.1.refs_0_), channel_id=1, source_target_pairs={{0,16},{8,24},{16,0},{24,8},{1,17},{9,25},{17,1},{25,9},{2,18},{10... | collective-permute-start | bytes 4718600 | tf_op jit(solution)/shard_map/ppermute | solution.py:25
  307.0 100.6 %collective-permute-start = (bf16[8,4,64,384]{3,2,1,0:T(8,128)(2,1)S(1)}, bf16[8,4,64,384]{3,2,1,0:T(8,128)(2,1)}, u32[]{:S(2)}, u32[]{:S(2)}) collective-permute-start(bf16[8,4,64,384]{3,2,1,0:T(8,128)(2,1)S(1)} %all-to-all-done.refs_0_), channel_id=1, source_target_pairs={{0,16},{8,24},{16,0},{24,8},{1,17},{9,25},{17,1},{25,9},{2,18},{10... | collective-permute-start | bytes 4718600 | tf_op jit(solution)/shard_map/ppermute | solution.py:25
  310.4 98.5 %collective-permute-start.11 = (bf16[8,4,64,384]{3,2,1,0:T(8,128)(2,1)}, bf16[8,4,64,384]{3,2,1,0:T(8,128)(2,1)}, u32[]{:S(2)}, u32[]{:S(2)}) collective-permute-start(bf16[8,4,64,384]{3,2,1,0:T(8,128)(2,1)} %collective-permute-done.10.refs_2_), channel_id=1, source_target_pairs={{0,8},{8,0},{16,24},{24,16},{1,9},{9,1},{17,25},{25,17},{2,10},{10... | collective-permute-start | bytes 4718600 | tf_op jit(solution)/shard_map/ppermute | solution.py:25
  340.7 81.2 %collective-permute-start.8 = (bf16[8,4,64,384]{3,2,1,0:T(8,128)(2,1)}, bf16[8,4,64,384]{3,2,1,0:T(8,128)(2,1)}, u32[]{:S(2)}, u32[]{:S(2)}) collective-permute-start(bf16[8,4,64,384]{3,2,1,0:T(8,128)(2,1)} %collective-permute-done.7.refs_2_), channel_id=1, source_target_pairs={{0,8},{8,0},{16,24},{24,16},{1,9},{9,1},{17,25},{25,17},{2,10},{10... | collective-permute-start | bytes 4718600 | tf_op jit(solution)/shard_map/ppermute | solution.py:25
  361.0 74.8 %collective-permute-start.3 = (bf16[8,4,64,384]{3,2,1,0:T(8,128)(2,1)}, bf16[8,4,64,384]{3,2,1,0:T(8,128)(2,1)}, u32[]{:S(2)}, u32[]{:S(2)}) collective-permute-start(bf16[8,4,64,384]{3,2,1,0:T(8,128)(2,1)} %all-to-all-done.1.refs_0_), channel_id=1, source_target_pairs={{0,8},{8,0},{16,24},{24,16},{1,9},{9,1},{17,25},{25,17},{2,10},{10... | collective-permute-start | bytes 4718600 | tf_op jit(solution)/shard_map/ppermute | solution.py:25
  374.4 61.4 %collective-permute-start.5 = (bf16[8,4,64,384]{3,2,1,0:T(8,128)(2,1)}, bf16[8,4,64,384]{3,2,1,0:T(8,128)(2,1)}, u32[]{:S(2)}, u32[]{:S(2)}) collective-permute-start(bf16[8,4,64,384]{3,2,1,0:T(8,128)(2,1)} %collective-permute-done.4.refs_2_), channel_id=1, source_target_pairs={{0,8},{8,0},{16,24},{24,16},{1,9},{9,1},{17,25},{25,17},{2,10},{10... | collective-permute-start | bytes 4718600 | tf_op jit(solution)/shard_map/ppermute | solution.py:25
  407.6 40.5 %collective-permute-start.2 = (bf16[8,4,64,384]{3,2,1,0:T(8,128)(2,1)S(1)}, bf16[8,4,64,384]{3,2,1,0:T(8,128)(2,1)}, u32[]{:S(2)}, u32[]{:S(2)}) collective-permute-start(bf16[8,4,64,384]{3,2,1,0:T(8,128)(2,1)S(1)} %all-to-all-done.refs_0_), channel_id=1, source_target_pairs={{0,8},{8,0},{16,24},{24,16},{1,9},{9,1},{17,25},{25,17},{2,10},{10... | collective-permute-start | bytes 4718600 | tf_op jit(solution)/shard_map/ppermute | solution.py:25
  409.0 46.9 %collective-permute-start.1 = (bf16[8,4,64,384]{3,2,1,0:T(8,128)(2,1)}, bf16[8,4,64,384]{3,2,1,0:T(8,128)(2,1)}, u32[]{:S(2)}, u32[]{:S(2)}) collective-permute-start(bf16[8,4,64,384]{3,2,1,0:T(8,128)(2,1)} %collective-permute-done.refs_0_), channel_id=1, source_target_pairs={{0,8},{8,0},{16,24},{24,16},{1,9},{9,1},{17,25},{25,17},{2,10},{10... | collective-permute-start | bytes 4718600 | tf_op jit(solution)/shard_map/ppermute | solution.py:25
  421.9 53.7 %collective-permute-start.34 = (f32[4,96,128]{2,1,0:T(8,128)S(1)}, f32[4,96,128]{2,1,0:T(8,128)}, u32[]{:S(2)}, u32[]{:S(2)}) collective-permute-start(f32[4,96,128]{2,1,0:T(8,128)S(1)} %dynamic-slice_bitcast_fusion.2), channel_id=1, source_target_pairs={{0,1},{1,0},{2,3},{3,2},{4,5},{5,4},{6,7},{7,6},{8,9},{9,8},{10,11... | collective-permute-start | bytes 589832 | tf_op jit(solution)/shard_map/ppermute | solution.py:25
  465.8 15.0 %collective-permute-start.22 = (f32[4,96,384]{2,1,0:T(8,128)S(1)}, f32[4,96,384]{2,1,0:T(8,128)S(1)}, u32[]{:S(2)}, u32[]{:S(2)}) collective-permute-start(f32[4,96,384]{2,1,0:T(8,128)S(1)} %dynamic-slice_bitcast_fusion), channel_id=1, source_target_pairs={{0,1},{1,0},{2,3},{3,2},{4,5},{5,4},{6,7},{7,6},{8,9},{9,8},{10,11... | collective-permute-start | bytes 1769480 | tf_op jit(solution)/shard_map/ppermute | solution.py:25
  (37 other events, 957.0 us)

commit v2 on v1

--- a/solution.py
+++ b/solution.py
@@ -9,16 +9,19 @@
 from jax.sharding import PartitionSpec as P
 
 
-PHASES = (((0, 6), (0, 4, 8, 12, 16)), ((6, 8), (0, 8, 12, 16)))
+MAIN = ((0, 6, 0, 4), (0, 6, 4, 8), (0, 6, 8, 12), (0, 6, 12, 16), (6, 8, 12, 16))
+SHADOW = ((6, 8, 0, 4), (6, 8, 4, 8), (6, 8, 8, 12), None, None)
+SPLIT = 2
 
 
 def chunks_of(columns, rows):
-    found = []
-    for (a0, a1), cuts in PHASES:
-        cuts = sorted({c * rows // 16 for c in cuts})
-        for f0, f1 in zip(cuts, cuts[1:]):
-            found.append((a0 * columns // 8, a1 * columns // 8, f0, f1))
-    return found
+    found = {}
+    for n, pair in enumerate(zip(MAIN, SHADOW)):
+        for name, cut in zip((f"m{n}", f"q{n}"), pair):
+            if cut is not None:
+                a0, a1, f0, f1 = cut
+                found[name] = (a0 * columns // 8, a1 * columns // 8, f0 * rows // 16, f1 * rows // 16)
+    return {name: cut for name, cut in found.items() if cut[3] > cut[2]}
 
 
 def swap(value, axis, size, bit):
@@ -46,6 +49,29 @@
         partial = keep + swap(give, "virt", size, bit)
         bit *= 2
     return partial[0]
+
+
+def assemble_body(place_ref, *refs):
+    for k, ref in enumerate(refs[:-1]):
+
+        @pl.when(pl.program_id(0) == k)
+        def _(ref=ref):
+            refs[-1][...] = ref[...]
+
+
+def assemble(parts, place):
+    shape = parts[0].shape
+    rest = (0,) * (len(shape) - 1)
+    return pl.pallas_call(
+        assemble_body,
+        grid_spec=pltpu.PrefetchScalarGridSpec(
+            num_scalar_prefetch=1,
+            grid=(len(parts),),
+            in_specs=[pl.BlockSpec(shape, lambda i, q: (0, *rest)) for _ in parts],
+            out_specs=pl.BlockSpec(shape, lambda i, q: (q[0] ^ i, *rest)),
+        ),
+        out_shape=jax.ShapeDtypeStruct((len(parts), *shape[1:]), parts[0].dtype),
+    )(place[None].astype(jnp.int32), *parts)
 
 
 def pack_body(place_ref, select_ref, slab_ref, *out_refs, chunks):
@@ -91,12 +117,12 @@
 
 
 def ladder_body(place_ref, tau_ref, *refs, steps, count):
-    pieces, out_ref = refs[:count], refs[-1]
+    pieces, out_ref, left_ref = refs[:count], refs[-2], refs[-1]
     at = pl.program_id(0)
 
     @pl.when(at == 0)
     def _():
-        out_ref[...] = refs[count][...] if len(refs) > count + 1 else jnp.zeros_like(out_ref)
+        out_ref[...] = refs[count][...] if len(refs) > count + 2 else jnp.zeros_like(out_ref)
 
     for k, piece_ref in enumerate(pieces):
 
@@ -104,11 +130,12 @@
         def _(piece_ref=piece_ref):
             sources, taken, rows, columns = piece_ref.shape
             left = [piece_ref[:, f].reshape(sources * rows, columns) for f in range(taken)]
-            left = jnp.concatenate(left, 0)
-            right = tau_ref[...].reshape(left.shape[0], tau_ref.shape[-1])
-            out_ref[...] += lax.dot_general(
-                left, right, (((0,), (0,)), ((), ())), preferred_element_type=jnp.float32
-            )
+            left_ref[...] = jnp.concatenate(left, 0)
+
+    right = tau_ref[...].reshape(left_ref.shape[0], tau_ref.shape[-1])
+    out_ref[...] += lax.dot_general(
+        left_ref[...], right, (((0,), (0,)), ((), ())), preferred_element_type=jnp.float32
+    )
 
 
 def ladder(tau, pieces, running, places, first, roots):
@@ -137,12 +164,13 @@
             in_specs=[
                 pl.BlockSpec(
                     (step, total, pairs),
-                    lambda i, q: ((q[i // steps] * span + first) // step + i % steps, 0, 0),
+                    lambda i, q: (q[i // steps] + i % steps, 0, 0),
                 ),
                 *[piece_spec(k) for k in range(count)],
                 *[whole for _ in given],
             ],
             out_specs=whole,
+            scratch_shapes=[pltpu.VMEM((step * sources * rows, columns), tau.dtype)],
         ),
         out_shape=jax.ShapeDtypeStruct((columns, pairs), jnp.float32),
         input_output_aliases={2 + count: 0} if given else {},
@@ -151,7 +179,7 @@
             bytes_accessed=2 * count * sources * taken * rows * (columns + pairs),
             transcendentals=0,
         ),
-    )(jnp.stack(places).astype(jnp.int32), tau, *pieces, *given)
+    )((jnp.stack(places).astype(jnp.int32) * span + first) // step, tau, *pieces, *given)
 
 
 def on_device(sizes, r2, tau, w_vvv, w_oooo, w_ovoo, fock_oo, fock_vv, r1):
@@ -164,25 +192,31 @@
     pair_rows = w_oooo.shape[0]
     rq = pair_rows // roots
 
+    def exchange(send):
+        parts = []
+        for key in range(virts):
+            piece = lax.dynamic_index_in_dim(send, virt ^ key, 0)
+            if key:
+                piece = lax.ppermute(piece, "virt", [(k, k ^ key) for k in range(virts)])
+            parts.append(piece)
+        return assemble(parts, virt)
+
     chunks = chunks_of(columns, fblock // roots)
-    sends = pack(w_vvv, virts, roots, root, chunks)
-    arrived = []
-    for send in sends:
-        arrived.append(lax.all_to_all(send, "virt", 0, 0, tiled=True))
+    sends = pack(w_vvv, virts, roots, root, list(chunks.values()))
+    arrived = {}
+    for name, send in zip(chunks, sends):
+        if name[0] == "m":
+            arrived[name] = lax.all_to_all(send, "virt", 0, 0, tiled=True)
+        else:
+            arrived[name] = exchange(send)
 
     own_rows = lax.dynamic_slice_in_dim(w_oooo, root * rq, rq, 0)
     small = jnp.concatenate([r2, own_rows], 0)
     inner = small.shape[1] // virts
     small = small.reshape(block + rq, virts, inner).transpose(1, 0, 2)
-    r2_part = jnp.zeros((virts, block, inner), r2.dtype)
-    rows_part = jnp.zeros((virts, rq, inner), r2.dtype)
-    for key in range(virts):
-        piece = lax.dynamic_index_in_dim(small, virt ^ key, 0)
-        if key:
-            piece = lax.ppermute(piece, "virt", [(k, k ^ key) for k in range(virts)])
-        r2_part = lax.dynamic_update_slice(r2_part, piece[:, :block], (virt ^ key, 0, 0))
-        rows_part = lax.dynamic_update_slice(rows_part, piece[:, block:], (virt ^ key, 0, 0))
-    r2_part = r2_part.reshape(columns, inner)
+    small = exchange(small)
+    r2_part = small[:, :block].reshape(columns, inner)
+    rows_part = small[:, block:]
     rows_of = spread(rows_part, roots)
     oooo_part = jnp.zeros((virts, roots, rq, inner), r2.dtype)
     for key, part in rows_of.items():
@@ -207,22 +241,26 @@
 
     running = {}
     results = {}
-    for index, (a0, a1, f0, f1) in enumerate(chunks):
-        held = spread(arrived[index], roots)
-        for keys in groups_of(index, len(chunks), roots):
+    left = {}
+    for a0, _, f0, f1 in chunks.values():
+        left[a0] = left.get(a0, 0) + f1 - f0
+    for name, (a0, a1, f0, f1) in chunks.items():
+        held = spread(arrived[name], roots)
+        for keys in groups_of(name, roots):
             running[a0] = ladder(
                 tau, [held[k] for k in keys], running.get(a0), [root ^ k for k in keys], f0, roots
             )
-        if f1 == fblock // roots:
+        left[a0] -= f1 - f0
+        if not left[a0]:
             partial = running[a0].T + extra[:, a0:a1]
             summed = scatter_sum(partial.reshape(virts, pair_rows, a1 - a0), virts)
             results[a0] = summed - singles[:, a0:a1]
     return jnp.concatenate([results[a0] for a0 in sorted(results)], 1)
 
 
-def groups_of(index, count, roots):
+def groups_of(name, roots):
     keys = list(range(roots))
-    if index + 4 < count:
+    if name[0] == "q" or int(name[1:]) + SPLIT < len(MAIN):
         return [keys]
     return [keys[: roots // 2], keys[roots // 2 :]]
 

time: 506 us -> 534 us (1.055); the launches traced: 499 us -> 533 us
  starting transfers between devices: 50.7 us -> 84.2 us
  Pallas kernels: 101 us -> 116 us
  local copies, waits for them, and re-layouts: 31.9 us -> 20 us
  blocking collectives: 109 us -> 103 us
    ppermute x7 -> x28, waiting for transfers between devices: 16.1 us -> 66.5 us  [exchange(): piece = lax.ppermute(piece, 'virt', [(k, k ^ key) for k in range(virts)])]
    ppermute x7 -> x28, starting transfers between devices: 15.6 us -> 57.6 us  [exchange(): piece = lax.ppermute(piece, 'virt', [(k, k ^ key) for k in range(virts)])]
    all_to_all x3 -> x2, waiting for transfers between devices: 36.1 us -> 0.01 us  [on_device(): arrived[name] = lax.all_to_all(send, 'virt', 0, 0, tiled=True)]
    dynamic_update_slice x16 -> x0, local copies, waits for them, and re-layouts: 16.2 us -> none  [the longest x8 10.9 us: on_device(): lax.dynamic_update_slice(r2_part, piece[:, :block], (virt ^ key, 0, 0))]
    pallas_call x0 -> x4, Pallas kernels: none -> 14.7 us  [assemble(): pl.pallas_call(assemble_body, grid_spec=pltpu.PrefetchScalarGridSpec(num_...]
    ppermute x30 -> x33, waiting for transfers between devices: 130 us -> 118 us  [swap(): return lax.ppermute(value, axis, [(k, k ^ bit) for k in range(size)])]
    all_to_all x4 -> x3, blocking collectives: 109 us -> 103 us  [on_device(): arrived[name] = lax.all_to_all(send, 'virt', 0, 0, tiled=True)]
    all_to_all x3 -> x2, starting transfers between devices: 12.6 us -> 7.47 us  [on_device(): arrived[name] = lax.all_to_all(send, 'virt', 0, 0, tiled=True)]
  transfers between devices with their start and end apart: 40 -> 63, of which waited for: 14 -> 19; matrix products, arithmetic and copies ran while one was open for 11% -> 8% of each run, Pallas kernels for 18% -> 20%
where the time goes in v2:
time: 534 us; the launch traced here: 533 us
  waiting for transfers between devices  185 us (35%)
  Pallas kernels  116 us (22%)
  blocking collectives  103 us (19%)
  starting transfers between devices  84.2 us (16%)
  local copies, waits for them, and re-layouts  20 us (4%)
  matrix products  17.6 us (3%)
  other arithmetic  6.96 us (1%)
    ppermute x33, waiting for transfers between devices, swap(): return lax.ppermute(value, axis, [(k, k ^ bit) for k in range(size)])  118 us
    all_to_all x3, blocking collectives, on_device(): arrived[name] = lax.all_to_all(send, 'virt', 0, 0, tiled=True)  103 us
    pallas_call x10, Pallas kernels, ladder(): pl.pallas_call(functools.partial(ladder_body, steps=steps, count=count),...  91 us
    ppermute x28, waiting for transfers between devices, exchange(): piece = lax.ppermute(piece, 'virt', [(k, k ^ key) for k in range(virts)])  66.5 us
    ppermute x28, starting transfers between devices, exchange(): piece = lax.ppermute(piece, 'virt', [(k, k ^ key) for k in range(virts)])  57.6 us
    ppermute x33, starting transfers between devices, swap(): return lax.ppermute(value, axis, [(k, k ^ bit) for k in range(size)])  19.1 us
    pallas_call x4, Pallas kernels, assemble(): pl.pallas_call(assemble_body, grid_spec=pltpu.PrefetchScalarGridSpec(num_...  14.7 us
  transfers between devices with their start and end apart: 63, of which 19 were waited for; matrix products, arithmetic and copies ran while one was open for 8% of the time, Pallas kernels for 20%

profile of v2, /device:TPU:0, one launch (start us, length us, event | category | flops | bytes accessed | tf_op | source)
XLA Modules:
  0.0 532.9 jit_solution(12281750364729350465)
XLA Ops:
  0.0 10.3 %shard_map.91 = (bf16[8,4,64,384]{3,2,1,0:T(8,128)(2,1)}, bf16[8,4,64,128]{3,2,1,0:T(8,128)(2,1)}, bf16[8,4,64,384]{3,2,1,0:T(8,128)(2,1)}, bf16[8,4,64,128]{3,2...) custom-call(s32[1]{0:T(128)} %bitcast.2.place_ref, ...), custom_call_target="tpu_custom_call" | custom-call | flops 2147483648 | bytes 16777216 | tf_op jit(solution)/shard_map/pallas_call | solution.py:99
  10.3 21.9 %all_to_all.25.refs_0_ = bf16[8,4,64,128]{3,2,1,0:T(8,128)(2,1)} all-to-all(bf16[8,4,64,128]{3,2,1,0:T(8,128)(2,1)} %get-tuple-element.17), channel_id=1, replica_groups=mesh['root'=4,'virt'=8] {'virt'}, dimensions={0} | all-to-all | bytes 1048576 | tf_op jit(solution)/shard_map/all_to_all | solution.py:209
  32.3 40.6 %all_to_all.26.refs_0_ = bf16[8,4,64,384]{3,2,1,0:T(8,128)(2,1)} all-to-all(bf16[8,4,64,384]{3,2,1,0:T(8,128)(2,1)} %get-tuple-element.14), channel_id=1, replica_groups=mesh['root'=4,'virt'=8] {'virt'}, dimensions={0} | all-to-all | bytes 3145728 | tf_op jit(solution)/shard_map/all_to_all | solution.py:209
  72.9 40.1 %all_to_all.27.refs_0_ = bf16[8,4,64,384]{3,2,1,0:T(8,128)(2,1)} all-to-all(bf16[8,4,64,384]{3,2,1,0:T(8,128)(2,1)S(1)} %copy-done.9), channel_id=1, replica_groups=mesh['root'=4,'virt'=8] {'virt'}, dimensions={0} | all-to-all | bytes 3145728 | tf_op jit(solution)/shard_map/all_to_all | solution.py:209
  117.5 4.6 collective-permute-start.54
  129.3 20.6 %collective-permute-done.54.refs_7_ = bf16[1,4,64,128]{3,2,1,0:T(8,128)(2,1)S(1)} collective-permute-done((bf16[1,4,64,128]{3,2,1,0:T(8,128)(2,1)}, bf16[1,4,64,128]{3,2,1,0:T(8,128)(2,1)S(1)}, u32[]{:S(2)}, u32[]{:S(2)}) %collective-permute-start.54) | collective-permute-done | bytes 65568 | tf_op jit(solution)/shard_map/ppermute | solution.py:200
  150.4 13.6 %collective-permute-start.13 = (bf16[1,88,512]{2,1,0:T(8,128)(2,1)S(1)}, bf16[1,88,512]{2,1,0:T(8,128)(2,1)}, u32[]{:S(2)}, u32[]{:S(2)}) collective-permute-start(bf16[1,88,512]{2,1,0:T(8,128)(2,1)S(1)} %bitcast.129), channel_id=1, source_target_pairs={{0,2},{1,3},{2,0},{3,1},{4,6},{5,7},{6,4},{7,5},{8,10},{9,11},{10,... | collective-permute-start | bytes 270344 | tf_op jit(solution)/shard_map/ppermute | solution.py:200
  169.5 3.8 all-to-all-start
  187.0 34.1 %collective-permute-done.15.refs_4_ = bf16[1,88,512]{2,1,0:T(8,128)(2,1)} collective-permute-done((bf16[1,88,512]{2,1,0:T(8,128)(2,1)S(1)}, bf16[1,88,512]{2,1,0:T(8,128)(2,1)}, u32[]{:S(2)}, u32[]{:S(2)}) %collective-permute-start.15) | collective-permute-done | bytes 90144 | tf_op jit(solution)/shard_map/ppermute | solution.py:200
  226.1 5.0 collective-permute-start.31
  231.1 3.8 shard_map.97
  277.6 6.0 %collective-permute-done.46.refs_2_ = bf16[8,4,64,128]{3,2,1,0:T(8,128)(2,1)} collective-permute-done((bf16[8,4,64,128]{3,2,1,0:T(8,128)(2,1)}, bf16[8,4,64,128]{3,2,1,0:T(8,128)(2,1)}, u32[]{:S(2)}, u32[]{:S(2)}) %collective-permute-start.46) | collective-permute-done | bytes 524320 | tf_op jit(solution)/shard_map/ppermute | solution.py:28
  283.6 8.3 %collective-permute-done.36.refs_2_ = bf16[8,4,64,128]{3,2,1,0:T(8,128)(2,1)} collective-permute-done((bf16[8,4,64,128]{3,2,1,0:T(8,128)(2,1)}, bf16[8,4,64,128]{3,2,1,0:T(8,128)(2,1)}, u32[]{:S(2)}, u32[]{:S(2)}) %collective-permute-start.36) | collective-permute-done | bytes 524320 | tf_op jit(solution)/shard_map/ppermute | solution.py:28
  297.8 9.2 %collective-permute-done.25.refs_0_ = bf16[8,4,64,128]{3,2,1,0:T(8,128)(2,1)} collective-permute-done((bf16[8,4,64,128]{3,2,1,0:T(8,128)(2,1)}, bf16[8,4,64,128]{3,2,1,0:T(8,128)(2,1)}, u32[]{:S(2)}, u32[]{:S(2)}) %collective-permute-start.25) | collective-permute-done | bytes 524320 | tf_op jit(solution)/shard_map/ppermute | solution.py:28
  314.7 26.0 %collective-permute-done.10.refs_2_ = bf16[8,4,64,384]{3,2,1,0:T(8,128)(2,1)} collective-permute-done((bf16[8,4,64,384]{3,2,1,0:T(8,128)(2,1)}, bf16[8,4,64,384]{3,2,1,0:T(8,128)(2,1)}, u32[]{:S(2)}, u32[]{:S(2)}) %collective-permute-start.10) | collective-permute-done | bytes 1572896 | tf_op jit(solution)/shard_map/ppermute | solution.py:28
  346.1 28.3 %collective-permute-done.7.refs_2_ = bf16[8,4,64,384]{3,2,1,0:T(8,128)(2,1)} collective-permute-done((bf16[8,4,64,384]{3,2,1,0:T(8,128)(2,1)}, bf16[8,4,64,384]{3,2,1,0:T(8,128)(2,1)}, u32[]{:S(2)}, u32[]{:S(2)}) %collective-permute-start.7) | collective-permute-done | bytes 1572896 | tf_op jit(solution)/shard_map/ppermute | solution.py:28
  374.4 3.9 fusion.3
  378.3 8.5 %shard_map.101.refs_4_ = f32[128,768]{1,0:T(8,128)} custom-call(s32[4]{0:T(128)} %get-tuple-element.21.place_ref, bf16[64,512,768]{2,1,0:T(8,128)(2,1)} %tau_ref.19, bf16[8,4,64,128]{3,2,1,0:T(8,128)(2,1)} %shard_map.100.refs_0_, bf16[8,4,64,128]{3,2,1,0:T(8,128)(2,1)} %collective-permute-done.55.refs_1_, bf16[8,4,64,128]{3,2,1,0:T(8,128)(2,1)} %copy-done.10, ...), custom_call_target="tpu_custom_call" | custom-call | flops 1610612736 | bytes 14680064 | tf_op jit(solution)/shard_map/pallas_call | solution.py:159
  386.8 8.6 %shard_map.102.refs_4_ = f32[128,768]{1,0:T(8,128)} custom-call(s32[4]{0:T(128)} %get-tuple-element.55.place_ref, bf16[64,512,768]{2,1,0:T(8,128)(2,1)} %tau_ref.19, bf16[8,4,64,128]{3,2,1,0:T(8,128)(2,1)} %shard_map.99.refs_0_, bf16[8,4,64,128]{3,2,1,0:T(8,128)(2,1)} %collective-permute-done.45.refs_1_, ...), custom_call_target="tpu_custom_call", output_to_operand_aliasing={{}: (6, {})} | custom-call | flops 1610612736 | bytes 14680064 | tf_op jit(solution)/shard_map/pallas_call | solution.py:159
  395.9 12.2 %collective-permute-done.4.refs_2_ = bf16[8,4,64,384]{3,2,1,0:T(8,128)(2,1)} collective-permute-done((bf16[8,4,64,384]{3,2,1,0:T(8,128)(2,1)}, bf16[8,4,64,384]{3,2,1,0:T(8,128)(2,1)}, u32[]{:S(2)}, u32[]{:S(2)}) %collective-permute-start.4) | collective-permute-done | bytes 1572896 | tf_op jit(solution)/shard_map/ppermute | solution.py:28
  408.1 8.6 %shard_map.103.refs_2_ = f32[128,768]{1,0:T(8,128)} custom-call(s32[4]{0:T(128)} %get-tuple-element.56.place_ref, bf16[64,512,768]{2,1,0:T(8,128)(2,1)} %tau_ref.19, bf16[8,4,64,128]{3,2,1,0:T(8,128)(2,1)} %shard_map.98.refs_0_, bf16[8,4,64,128]{3,2,1,0:T(8,128)(2,1)} %collective-permute-done.35.refs_1_, ...), custom_call_target="tpu_custom_call", output_to_operand_aliasing={{}: (6, {})} | custom-call | flops 1610612736 | bytes 14680064 | tf_op jit(solution)/shard_map/pallas_call | solution.py:159
  416.7 5.5 %shard_map.104.refs_2_ = f32[128,768]{1,0:T(8,128)} custom-call(s32[2]{0:T(128)} %and_select_fusion.3.place_ref, bf16[64,512,768]{2,1,0:T(8,128)(2,1)} %tau_ref.19, bf16[8,4,64,128]{3,2,1,0:T(8,128)(2,1)} %all_to_all.25.refs_0_, bf16[8,4,64,128]{3,2,1,0:T(8,128)(2,1)} %copy-done.11, f32[128,768]{1,0:T(8,128)} %shard_map.103.refs_2_), custom_call_target="tpu_custom_call", output_to_operand_aliasing={{}: (4, {})} | custom-call | flops 805306368 | bytes 7340032 | tf_op jit(solution)/shard_map/pallas_call | solution.py:159
  422.2 5.5 %shard_map.105 = f32[128,768]{1,0:T(8,128)} custom-call(s32[2]{0:T(128)} %and_select_fusion.4.place_ref, bf16[64,512,768]{2,1,0:T(8,128)(2,1)} %tau_ref.19, bf16[8,4,64,128]{3,2,1,0:T(8,128)(2,1)} %collective-permute-done.25.refs_0_, bf16[8,4,64,128]{3,2,1,0:T(8,128)(2,1)} %collective-permute-done.26.refs_1_, ...), custom_call_target="tpu_custom_call", output_to_operand_aliasing={{}: (4, {})} | custom-call | flops 805306368 | bytes 7340032 | tf_op jit(solution)/shard_map/pallas_call | solution.py:159
  427.7 13.7 %collective-permute-done.refs_0_ = bf16[8,4,64,384]{3,2,1,0:T(8,128)(2,1)} collective-permute-done((bf16[8,4,64,384]{3,2,1,0:T(8,128)(2,1)S(1)}, bf16[8,4,64,384]{3,2,1,0:T(8,128)(2,1)}, u32[]{:S(2)}, u32[]{:S(2)}) %collective-permute-start) | collective-permute-done | bytes 1572896 | tf_op jit(solution)/shard_map/ppermute | solution.py:28
  443.3 12.6 %shard_map.92.refs_4_ = f32[384,768]{1,0:T(8,128)} custom-call(s32[4]{0:T(128)} %get-tuple-element.21.place_ref, bf16[64,512,768]{2,1,0:T(8,128)(2,1)} %tau_ref.19, bf16[8,4,64,384]{3,2,1,0:T(8,128)(2,1)} %copy-done.5, bf16[8,4,64,384]{3,2,1,0:T(8,128)(2,1)} %collective-permute-done.9.refs_1_, bf16[8,4,64,384]{3,2,1,0:T(8,128)(2,1)} %collective-permute-done.10.refs_2_, ...), custom_call_target="tpu_custom_call" | custom-call | flops 4831838208 | bytes 18874368 | tf_op jit(solution)/shard_map/pallas_call | solution.py:159
  457.0 12.6 %shard_map.93.refs_4_ = f32[384,768]{1,0:T(8,128)} custom-call(s32[4]{0:T(128)} %get-tuple-element.55.place_ref, bf16[64,512,768]{2,1,0:T(8,128)(2,1)} %tau_ref.19, bf16[8,4,64,384]{3,2,1,0:T(8,128)(2,1)} %all_to_all.27.refs_0_, bf16[8,4,64,384]{3,2,1,0:T(8,128)(2,1)} %collective-permute-done.6.refs_1_, ...), custom_call_target="tpu_custom_call", output_to_operand_aliasing={{}: (6, {})} | custom-call | flops 4831838208 | bytes 18874368 | tf_op jit(solution)/shard_map/pallas_call | solution.py:159
  469.6 12.7 %shard_map.94.refs_2_ = f32[384,768]{1,0:T(8,128)} custom-call(s32[4]{0:T(128)} %get-tuple-element.56.place_ref, bf16[64,512,768]{2,1,0:T(8,128)(2,1)} %tau_ref.19, bf16[8,4,64,384]{3,2,1,0:T(8,128)(2,1)} %all_to_all.26.refs_0_, bf16[8,4,64,384]{3,2,1,0:T(8,128)(2,1)} %collective-permute-done.3.refs_1_, ...), custom_call_target="tpu_custom_call", output_to_operand_aliasing={{}: (6, {})} | custom-call | flops 4831838208 | bytes 18874368 | tf_op jit(solution)/shard_map/pallas_call | solution.py:159
  482.2 8.2 %shard_map.95.refs_2_ = f32[384,768]{1,0:T(8,128)} custom-call(s32[2]{0:T(128)} %and_select_fusion.3.place_ref, bf16[64,512,768]{2,1,0:T(8,128)(2,1)} %tau_ref.19, bf16[8,4,64,384]{3,2,1,0:T(8,128)(2,1)} %copy-done.2, bf16[8,4,64,384]{3,2,1,0:T(8,128)(2,1)} %collective-permute-done.2.refs_1_, ...), custom_call_target="tpu_custom_call", output_to_operand_aliasing={{}: (4, {})} | custom-call | flops 2415919104 | bytes 9437184 | tf_op jit(solution)/shard_map/pallas_call | solution.py:159
  490.4 8.3 %shard_map.96 = f32[384,768]{1,0:T(8,128)} custom-call(s32[2]{0:T(128)} %and_select_fusion.4.place_ref, bf16[64,512,768]{2,1,0:T(8,128)(2,1)} %tau_ref.19, bf16[8,4,64,384]{3,2,1,0:T(8,128)(2,1)} %collective-permute-done.refs_0_, bf16[8,4,64,384]{3,2,1,0:T(8,128)(2,1)} %collective-permute-done.1.refs_1_, ...), custom_call_target="tpu_custom_call", output_to_operand_aliasing={{}: (4, {})} | custom-call | flops 2415919104 | bytes 9437184 | tf_op jit(solution)/shard_map/pallas_call | solution.py:159
  501.5 9.5 %fusion = f32[1,96,512]{2,0,1:T(1,128)S(1)} fusion(bf16[64]{0:T(256)(128)(2,1)S(1)} %copy-done.36, bf16[8,8,96,512]{3,2,1,0:T(8,128)(2,1)} %bitcast.135), kind=kOutput, calls=%fused_computation | convolution fusion | flops 6291456 | bytes 6488192 | tf_op jit(solution)/shard_map/dot_general | solution.py:238
  518.7 5.7 %collective-permute-done.23 = f32[2,96,384]{2,1,0:T(8,128)S(1)} collective-permute-done((f32[2,96,384]{2,1,0:T(8,128)S(1)}, f32[2,96,384]{2,1,0:T(8,128)S(1)}, u32[]{:S(2)}, u32[]{:S(2)}) %collective-permute-start.23) | collective-permute-done | bytes 294944 | tf_op jit(solution)/shard_map/ppermute | solution.py:28
  525.3 6.9 %collective-permute-done.24 = f32[1,96,384]{2,1,0:T(8,128)S(1)} collective-permute-done((f32[1,96,384]{2,1,0:T(8,128)S(1)}, f32[1,96,384]{2,1,0:T(8,128)S(1)}, u32[]{:S(2)}, u32[]{:S(2)}) %collective-permute-start.24) | collective-permute-done | bytes 147488 | tf_op jit(solution)/shard_map/ppermute | solution.py:28
  (241 shorter events, 113.3 us)
Async XLA Ops:
  112.9 55.4 %all-to-all-start.3 = ((bf16[8,4,64,384]{3,2,1,0:T(8,128)(2,1)}), bf16[8,4,64,384]{3,2,1,0:T(8,128)(2,1)S(1)}, u32[]{:S(2)}, u32[]{:S(2)}) async-start(bf16[8,4,64,384]{3,2,1,0:T(8,128)(2,1)} %get-tuple-element.16), calls=%async_computation.3 | async-start | bytes 3145728 | tf_op jit(solution)/shard_map/all_to_all | solution.py:209
  117.5 32.4 %collective-permute-start.54 = (bf16[1,4,64,128]{3,2,1,0:T(8,128)(2,1)}, bf16[1,4,64,128]{3,2,1,0:T(8,128)(2,1)S(1)}, u32[]{:S(2)}, u32[]{:S(2)}) collective-permute-start(bf16[1,4,64,128]{3,2,1,0:T(8,128)(2,1)} %get-tuple-element.31), channel_id=1, source_target_pairs={{0,7},{1,6},{2,5},{3,4},{4,3},{5,2},{6,1},{7,0},{8,15},{9,14},{10,... | collective-permute-start | bytes 196616 | tf_op jit(solution)/shard_map/ppermute | solution.py:200
  122.1 28.3 %collective-permute-start.53 = (bf16[1,4,64,128]{3,2,1,0:T(8,128)(2,1)}, bf16[1,4,64,128]{3,2,1,0:T(8,128)(2,1)}, u32[]{:S(2)}, u32[]{:S(2)}) collective-permute-start(bf16[1,4,64,128]{3,2,1,0:T(8,128)(2,1)} %get-tuple-element.32), channel_id=1, source_target_pairs={{0,6},{1,7},{2,4},{3,5},{4,2},{5,3},{6,0},{7,1},{8,14},{9,15},{10,... | collective-permute-start | bytes 196616 | tf_op jit(solution)/shard_map/ppermute | solution.py:200
  122.6 42.2 %collective-permute-start.52 = (bf16[1,4,64,128]{3,2,1,0:T(8,128)(2,1)}, bf16[1,4,64,128]{3,2,1,0:T(8,128)(2,1)}, u32[]{:S(2)}, u32[]{:S(2)}) collective-permute-start(bf16[1,4,64,128]{3,2,1,0:T(8,128)(2,1)} %get-tuple-element.33), channel_id=1, source_target_pairs={{0,5},{1,4},{2,7},{3,6},{4,1},{5,0},{6,3},{7,2},{8,13},{9,12},{10,... | collective-permute-start | bytes 196616 | tf_op jit(solution)/shard_map/ppermute | solution.py:200
  123.2 41.6 %collective-permute-start.51 = (bf16[1,4,64,128]{3,2,1,0:T(8,128)(2,1)}, bf16[1,4,64,128]{3,2,1,0:T(8,128)(2,1)}, u32[]{:S(2)}, u32[]{:S(2)}) collective-permute-start(bf16[1,4,64,128]{3,2,1,0:T(8,128)(2,1)} %get-tuple-element.34), channel_id=1, source_target_pairs={{0,4},{1,5},{2,6},{3,7},{4,0},{5,1},{6,2},{7,3},{8,12},{9,13},{10,... | collective-permute-start | bytes 196616 | tf_op jit(solution)/shard_map/ppermute | solution.py:200
  125.1 41.7 %collective-permute-start.50 = (bf16[1,4,64,128]{3,2,1,0:T(8,128)(2,1)S(1)}, bf16[1,4,64,128]{3,2,1,0:T(8,128)(2,1)}, u32[]{:S(2)}, u32[]{:S(2)}) collective-permute-start(bf16[1,4,64,128]{3,2,1,0:T(8,128)(2,1)S(1)} %get-tuple-element.35), channel_id=1, source_target_pairs={{0,3},{1,2},{2,1},{3,0},{4,7},{5,6},{6,5},{7,4},{8,11},{9,10},{10,... | collective-permute-start | bytes 196616 | tf_op jit(solution)/shard_map/ppermute | solution.py:200
  149.9 31.3 %collective-permute-start.12 = (bf16[1,88,512]{2,1,0:T(8,128)(2,1)S(1)}, bf16[1,88,512]{2,1,0:T(8,128)(2,1)}, u32[]{:S(2)}, u32[]{:S(2)}) collective-permute-start(bf16[1,88,512]{2,1,0:T(8,128)(2,1)S(1)} %bitcast.131), channel_id=1, source_target_pairs={{0,1},{1,0},{2,3},{3,2},{4,5},{5,4},{6,7},{7,6},{8,9},{9,8},{10,11... | collective-permute-start | bytes 270344 | tf_op jit(solution)/shard_map/ppermute | solution.py:200
  150.4 34.1 %collective-permute-start.13 = (bf16[1,88,512]{2,1,0:T(8,128)(2,1)S(1)}, bf16[1,88,512]{2,1,0:T(8,128)(2,1)}, u32[]{:S(2)}, u32[]{:S(2)}) collective-permute-start(bf16[1,88,512]{2,1,0:T(8,128)(2,1)S(1)} %bitcast.129), channel_id=1, source_target_pairs={{0,2},{1,3},{2,0},{3,1},{4,6},{5,7},{6,4},{7,5},{8,10},{9,11},{10,... | collective-permute-start | bytes 270344 | tf_op jit(solution)/shard_map/ppermute | solution.py:200
  164.8 19.9 %collective-permute-start.14 = (bf16[1,88,512]{2,1,0:T(8,128)(2,1)S(1)}, bf16[1,88,512]{2,1,0:T(8,128)(2,1)}, u32[]{:S(2)}, u32[]{:S(2)}) collective-permute-start(bf16[1,88,512]{2,1,0:T(8,128)(2,1)S(1)} %bitcast.128), channel_id=1, source_target_pairs={{0,3},{1,2},{2,1},{3,0},{4,7},{5,6},{6,5},{7,4},{8,11},{9,10},{10,... | collective-permute-start | bytes 270344 | tf_op jit(solution)/shard_map/ppermute | solution.py:200
  169.5 145.1 %all-to-all-start = ((bf16[8,4,64,384]{3,2,1,0:T(8,128)(2,1)}), bf16[8,4,64,384]{3,2,1,0:T(8,128)(2,1)S(1)}, u32[]{:S(2)}, u32[]{:S(2)}) async-start(bf16[8,4,64,384]{3,2,1,0:T(8,128)(2,1)} %get-tuple-element.13), calls=%async_computation | async-start | bytes 3145728 | tf_op jit(solution)/shard_map/all_to_all | solution.py:209
  173.4 47.7 %collective-permute-start.15 = (bf16[1,88,512]{2,1,0:T(8,128)(2,1)S(1)}, bf16[1,88,512]{2,1,0:T(8,128)(2,1)}, u32[]{:S(2)}, u32[]{:S(2)}) collective-permute-start(bf16[1,88,512]{2,1,0:T(8,128)(2,1)S(1)} %bitcast.134), channel_id=1, source_target_pairs={{0,4},{1,5},{2,6},{3,7},{4,0},{5,1},{6,2},{7,3},{8,12},{9,13},{10,... | collective-permute-start | bytes 270344 | tf_op jit(solution)/shard_map/ppermute | solution.py:200
  176.1 46.5 %collective-permute-start.16 = (bf16[1,88,512]{2,1,0:T(8,128)(2,1)S(1)}, bf16[1,88,512]{2,1,0:T(8,128)(2,1)}, u32[]{:S(2)}, u32[]{:S(2)}) collective-permute-start(bf16[1,88,512]{2,1,0:T(8,128)(2,1)S(1)} %bitcast.133), channel_id=1, source_target_pairs={{0,5},{1,4},{2,7},{3,6},{4,1},{5,0},{6,3},{7,2},{8,13},{9,12},{10,... | collective-permute-start | bytes 270344 | tf_op jit(solution)/shard_map/ppermute | solution.py:200
  181.2 42.7 %collective-permute-start.17 = (bf16[1,88,512]{2,1,0:T(8,128)(2,1)S(1)}, bf16[1,88,512]{2,1,0:T(8,128)(2,1)S(1)}, u32[]{:S(2)}, u32[]{:S(2)}) collective-permute-start(bf16[1,88,512]{2,1,0:T(8,128)(2,1)S(1)} %bitcast.132), channel_id=1, source_target_pairs={{0,6},{1,7},{2,4},{3,5},{4,2},{5,3},{6,0},{7,1},{8,14},{9,15},{10,... | collective-permute-start | bytes 270344 | tf_op jit(solution)/shard_map/ppermute | solution.py:200
  184.5 41.6 %collective-permute-start.18 = (bf16[1,88,512]{2,1,0:T(8,128)(2,1)S(1)}, bf16[1,88,512]{2,1,0:T(8,128)(2,1)S(1)}, u32[]{:S(2)}, u32[]{:S(2)}) collective-permute-start(bf16[1,88,512]{2,1,0:T(8,128)(2,1)S(1)} %bitcast.130), channel_id=1, source_target_pairs={{0,7},{1,6},{2,5},{3,4},{4,3},{5,2},{6,1},{7,0},{8,15},{9,14},{10,... | collective-permute-start | bytes 270344 | tf_op jit(solution)/shard_map/ppermute | solution.py:200
  184.8 89.4 %collective-permute-start.56 = (bf16[8,4,64,128]{3,2,1,0:T(8,128)(2,1)}, bf16[8,4,64,128]{3,2,1,0:T(8,128)(2,1)S(1)}, u32[]{:S(2)}, u32[]{:S(2)}) collective-permute-start(bf16[8,4,64,128]{3,2,1,0:T(8,128)(2,1)} %shard_map.100.refs_0_), channel_id=1, source_target_pairs={{0,16},{8,24},{16,0},{24,8},{1,17},{9,25},{17,1},{25,9},{2,18},{10... | collective-permute-start | bytes 1572872 | tf_op jit(solution)/shard_map/ppermute | solution.py:28
  239.2 17.7 %collective-permute-start.19 = (bf16[8,24,512]{2,1,0:T(8,128)(2,1)}, bf16[8,24,512]{2,1,0:T(8,128)(2,1)S(1)}, u32[]{:S(2)}, u32[]{:S(2)}) collective-permute-start(bf16[8,24,512]{2,1,0:T(8,128)(2,1)} %slice.37), channel_id=1, source_target_pairs={{0,16},{8,24},{16,0},{24,8},{1,17},{9,25},{17,1},{25,9},{2,18},{10... | collective-permute-start | bytes 589832 | tf_op jit(solution)/shard_map/ppermute | solution.py:28
  254.9 22.0 %collective-permute-start.55 = (bf16[8,4,64,128]{3,2,1,0:T(8,128)(2,1)}, bf16[8,4,64,128]{3,2,1,0:T(8,128)(2,1)}, u32[]{:S(2)}, u32[]{:S(2)}) collective-permute-start(bf16[8,4,64,128]{3,2,1,0:T(8,128)(2,1)} %shard_map.100.refs_0_), channel_id=1, source_target_pairs={{0,8},{8,0},{16,24},{24,16},{1,9},{9,1},{17,25},{25,17},{2,10},{10... | collective-permute-start | bytes 1572872 | tf_op jit(solution)/shard_map/ppermute | solution.py:28
  272.6 19.2 %collective-permute-start.36 = (bf16[8,4,64,128]{3,2,1,0:T(8,128)(2,1)}, bf16[8,4,64,128]{3,2,1,0:T(8,128)(2,1)}, u32[]{:S(2)}, u32[]{:S(2)}) collective-permute-start(bf16[8,4,64,128]{3,2,1,0:T(8,128)(2,1)} %shard_map.98.refs_0_), channel_id=1, source_target_pairs={{0,16},{8,24},{16,0},{24,8},{1,17},{9,25},{17,1},{25,9},{2,18},{10... | collective-permute-start | bytes 1572872 | tf_op jit(solution)/shard_map/ppermute | solution.py:28
  276.8 18.9 %collective-permute-start.57 = (bf16[8,4,64,128]{3,2,1,0:T(8,128)(2,1)}, bf16[8,4,64,128]{3,2,1,0:T(8,128)(2,1)}, u32[]{:S(2)}, u32[]{:S(2)}) collective-permute-start(bf16[8,4,64,128]{3,2,1,0:T(8,128)(2,1)} %copy-done.10), channel_id=1, source_target_pairs={{0,8},{8,0},{16,24},{24,16},{1,9},{9,1},{17,25},{25,17},{2,10},{10... | collective-permute-start | bytes 1572872 | tf_op jit(solution)/shard_map/ppermute | solution.py:28
  292.4 48.3 %collective-permute-start.10 = (bf16[8,4,64,384]{3,2,1,0:T(8,128)(2,1)}, bf16[8,4,64,384]{3,2,1,0:T(8,128)(2,1)}, u32[]{:S(2)}, u32[]{:S(2)}) collective-permute-start(bf16[8,4,64,384]{3,2,1,0:T(8,128)(2,1)} %copy-done.5), channel_id=1, source_target_pairs={{0,16},{8,24},{16,0},{24,8},{1,17},{9,25},{17,1},{25,9},{2,18},{10... | collective-permute-start | bytes 4718600 | tf_op jit(solution)/shard_map/ppermute | solution.py:28
  295.7 48.7 %collective-permute-start.9 = (bf16[8,4,64,384]{3,2,1,0:T(8,128)(2,1)}, bf16[8,4,64,384]{3,2,1,0:T(8,128)(2,1)}, u32[]{:S(2)}, u32[]{:S(2)}) collective-permute-start(bf16[8,4,64,384]{3,2,1,0:T(8,128)(2,1)} %copy-done.5), channel_id=1, source_target_pairs={{0,8},{8,0},{16,24},{24,16},{1,9},{9,1},{17,25},{25,17},{2,10},{10... | collective-permute-start | bytes 4718600 | tf_op jit(solution)/shard_map/ppermute | solution.py:28
  296.3 78.0 %collective-permute-start.7 = (bf16[8,4,64,384]{3,2,1,0:T(8,128)(2,1)}, bf16[8,4,64,384]{3,2,1,0:T(8,128)(2,1)}, u32[]{:S(2)}, u32[]{:S(2)}) collective-permute-start(bf16[8,4,64,384]{3,2,1,0:T(8,128)(2,1)} %all_to_all.27.refs_0_), channel_id=1, source_target_pairs={{0,16},{8,24},{16,0},{24,8},{1,17},{9,25},{17,1},{25,9},{2,18},{10... | collective-permute-start | bytes 4718600 | tf_op jit(solution)/shard_map/ppermute | solution.py:28
  311.8 83.6 %collective-permute-start.6 = (bf16[8,4,64,384]{3,2,1,0:T(8,128)(2,1)}, bf16[8,4,64,384]{3,2,1,0:T(8,128)(2,1)}, u32[]{:S(2)}, u32[]{:S(2)}) collective-permute-start(bf16[8,4,64,384]{3,2,1,0:T(8,128)(2,1)} %all_to_all.27.refs_0_), channel_id=1, source_target_pairs={{0,8},{8,0},{16,24},{24,16},{1,9},{9,1},{17,25},{25,17},{2,10},{10... | collective-permute-start | bytes 4718600 | tf_op jit(solution)/shard_map/ppermute | solution.py:28
  312.4 95.7 %collective-permute-start.4 = (bf16[8,4,64,384]{3,2,1,0:T(8,128)(2,1)}, bf16[8,4,64,384]{3,2,1,0:T(8,128)(2,1)}, u32[]{:S(2)}, u32[]{:S(2)}) collective-permute-start(bf16[8,4,64,384]{3,2,1,0:T(8,128)(2,1)} %all_to_all.26.refs_0_), channel_id=1, source_target_pairs={{0,16},{8,24},{16,0},{24,8},{1,17},{9,25},{17,1},{25,9},{2,18},{10... | collective-permute-start | bytes 4718600 | tf_op jit(solution)/shard_map/ppermute | solution.py:28
  340.7 100.7 %collective-permute-start = (bf16[8,4,64,384]{3,2,1,0:T(8,128)(2,1)S(1)}, bf16[8,4,64,384]{3,2,1,0:T(8,128)(2,1)}, u32[]{:S(2)}, u32[]{:S(2)}) collective-permute-start(bf16[8,4,64,384]{3,2,1,0:T(8,128)(2,1)S(1)} %all-to-all-done.refs_0_), channel_id=1, source_target_pairs={{0,16},{8,24},{16,0},{24,8},{1,17},{9,25},{17,1},{25,9},{2,18},{10... | collective-permute-start | bytes 4718600 | tf_op jit(solution)/shard_map/ppermute | solution.py:28
  344.5 98.2 %collective-permute-start.11 = (bf16[8,4,64,384]{3,2,1,0:T(8,128)(2,1)}, bf16[8,4,64,384]{3,2,1,0:T(8,128)(2,1)}, u32[]{:S(2)}, u32[]{:S(2)}) collective-permute-start(bf16[8,4,64,384]{3,2,1,0:T(8,128)(2,1)} %collective-permute-done.10.refs_2_), channel_id=1, source_target_pairs={{0,8},{8,0},{16,24},{24,16},{1,9},{9,1},{17,25},{25,17},{2,10},{10... | collective-permute-start | bytes 4718600 | tf_op jit(solution)/shard_map/ppermute | solution.py:28
  374.4 81.5 %collective-permute-start.8 = (bf16[8,4,64,384]{3,2,1,0:T(8,128)(2,1)}, bf16[8,4,64,384]{3,2,1,0:T(8,128)(2,1)}, u32[]{:S(2)}, u32[]{:S(2)}) collective-permute-start(bf16[8,4,64,384]{3,2,1,0:T(8,128)(2,1)} %collective-permute-done.7.refs_2_), channel_id=1, source_target_pairs={{0,8},{8,0},{16,24},{24,16},{1,9},{9,1},{17,25},{25,17},{2,10},{10... | collective-permute-start | bytes 4718600 | tf_op jit(solution)/shard_map/ppermute | solution.py:28
  395.4 74.2 %collective-permute-start.3 = (bf16[8,4,64,384]{3,2,1,0:T(8,128)(2,1)}, bf16[8,4,64,384]{3,2,1,0:T(8,128)(2,1)}, u32[]{:S(2)}, u32[]{:S(2)}) collective-permute-start(bf16[8,4,64,384]{3,2,1,0:T(8,128)(2,1)} %all_to_all.26.refs_0_), channel_id=1, source_target_pairs={{0,8},{8,0},{16,24},{24,16},{1,9},{9,1},{17,25},{25,17},{2,10},{10... | collective-permute-start | bytes 4718600 | tf_op jit(solution)/shard_map/ppermute | solution.py:28
  408.1 61.5 %collective-permute-start.5 = (bf16[8,4,64,384]{3,2,1,0:T(8,128)(2,1)}, bf16[8,4,64,384]{3,2,1,0:T(8,128)(2,1)}, u32[]{:S(2)}, u32[]{:S(2)}) collective-permute-start(bf16[8,4,64,384]{3,2,1,0:T(8,128)(2,1)} %collective-permute-done.4.refs_2_), channel_id=1, source_target_pairs={{0,8},{8,0},{16,24},{24,16},{1,9},{9,1},{17,25},{25,17},{2,10},{10... | collective-permute-start | bytes 4718600 | tf_op jit(solution)/shard_map/ppermute | solution.py:28
  441.3 40.9 %collective-permute-start.2 = (bf16[8,4,64,384]{3,2,1,0:T(8,128)(2,1)S(1)}, bf16[8,4,64,384]{3,2,1,0:T(8,128)(2,1)}, u32[]{:S(2)}, u32[]{:S(2)}) collective-permute-start(bf16[8,4,64,384]{3,2,1,0:T(8,128)(2,1)S(1)} %all-to-all-done.refs_0_), channel_id=1, source_target_pairs={{0,8},{8,0},{16,24},{24,16},{1,9},{9,1},{17,25},{25,17},{2,10},{10... | collective-permute-start | bytes 4718600 | tf_op jit(solution)/shard_map/ppermute | solution.py:28
  442.7 47.7 %collective-permute-start.1 = (bf16[8,4,64,384]{3,2,1,0:T(8,128)(2,1)}, bf16[8,4,64,384]{3,2,1,0:T(8,128)(2,1)}, u32[]{:S(2)}, u32[]{:S(2)}) collective-permute-start(bf16[8,4,64,384]{3,2,1,0:T(8,128)(2,1)} %collective-permute-done.refs_0_), channel_id=1, source_target_pairs={{0,8},{8,0},{16,24},{24,16},{1,9},{9,1},{17,25},{25,17},{2,10},{10... | collective-permute-start | bytes 4718600 | tf_op jit(solution)/shard_map/ppermute | solution.py:28
  455.9 55.2 %collective-permute-start.58 = (f32[4,96,128]{2,1,0:T(8,128)S(1)}, f32[4,96,128]{2,1,0:T(8,128)}, u32[]{:S(2)}, u32[]{:S(2)}) collective-permute-start(f32[4,96,128]{2,1,0:T(8,128)S(1)} %dynamic-slice_bitcast_fusion.2), channel_id=1, source_target_pairs={{0,1},{1,0},{2,3},{3,2},{4,5},{5,4},{6,7},{7,6},{8,9},{9,8},{10,11... | collective-permute-start | bytes 589832 | tf_op jit(solution)/shard_map/ppermute | solution.py:28
  (69 other events, 1089.9 us)
